TPU v7x, 16 devices: a whole 2x2x2 slice. The times are simulated.
16 devices in a mesh: t: 4 (over z, y), v: 4 (over x, core).
Axes of the slice: x: 2, y: 2, z: 2, core: 2. Of those that a mesh axis runs over, the one named last changes fastest.
Arguments:
- hidden_in: bfloat16 [1024, 2304], replicated
- seq_lens: int32 [1024], replicated
- target: int32 [1024], replicated
- g_attn_pre: bfloat16 [2304], replicated
- w_q: bfloat16 [2304, 2048], P(None, 't')
- w_k: bfloat16 [2304, 1024], P(None, 't')
- w_v: bfloat16 [2304, 1024], P(None, 't')
- w_o: bfloat16 [2048, 2304], P('t')
- g_attn_post: bfloat16 [2304], replicated
- g_mlp_pre: bfloat16 [2304], replicated
- w_gate: bfloat16 [2304, 9216], P(None, 't')
- w_up: bfloat16 [2304, 9216], P(None, 't')
- w_down: bfloat16 [9216, 2304], P('t')
- g_mlp_post: bfloat16 [2304], replicated
- g_final: bfloat16 [2304], replicated
- k_cache: bfloat16 [1024, 32, 4, 256], P(None, None, 't')
- v_cache: bfloat16 [1024, 32, 4, 256], P(None, None, 't')
- embed_table: bfloat16 [256000, 2304], P(('v', 't'))
Outputs:
- output 1: float32 [1024], replicated
- output 2: bfloat16 [1024, 2304], replicated
All inputs are finite; a program needn't handle non-finite values.
Results may differ from a plain program's by a relative error of at most 0.00785292.
Values sent between devices are 32-bit elements.
A program may use at most 1 GiB of HBM per device.

v0:
```python
import jax
import jax.numpy as jnp
from jax import lax
from jax.sharding import PartitionSpec as P

ATTN_CAP = 50.0
FINAL_CAP = 30.0
NORM_EPS = 1e-6
ROPE_BASE = 10000.0


def rms_norm(values, gain_vec):
    x_f32 = values.astype(jnp.float32)
    scaled = x_f32 * lax.rsqrt(jnp.mean(x_f32 * x_f32, axis=-1, keepdims=True) + NORM_EPS)
    return scaled * (1.0 + gain_vec.astype(jnp.float32))


def rotary(values, positions):
    half_dim = values.shape[-1] // 2
    inv_freq = ROPE_BASE ** (-2.0 * jnp.arange(half_dim, dtype=jnp.float32) / values.shape[-1])
    angles = positions.astype(jnp.float32)[:, None] * inv_freq[None, :]
    angles = angles.reshape((values.shape[0],) + (1,) * (values.ndim - 2) + (half_dim,))
    cos_t = jnp.cos(angles)
    sin_t = jnp.sin(angles)
    x_low = values[..., :half_dim]
    x_high = values[..., half_dim:]
    return jnp.concatenate([x_low * cos_t - x_high * sin_t, x_high * cos_t + x_low * sin_t], axis=-1)


def attention(normed, seq_lens, w_q, w_k, w_v, k_cache, v_cache):
    tokens, ctx_len, kv_heads, head_dim = k_cache.shape
    group_size = w_q.shape[1] // (kv_heads * head_dim)
    score_scale = head_dim ** -0.5
    q_rot = rotary(jnp.dot(normed, w_q, preferred_element_type=jnp.float32).reshape(tokens, kv_heads, group_size, head_dim), seq_lens).astype(jnp.bfloat16)
    k_rot = rotary(jnp.dot(normed, w_k, preferred_element_type=jnp.float32).reshape(tokens, kv_heads, head_dim), seq_lens).astype(jnp.bfloat16)
    v_new = jnp.dot(normed, w_v, preferred_element_type=jnp.float32).astype(jnp.bfloat16).reshape(tokens, kv_heads, head_dim)
    s_cache = jnp.einsum('nkgd,ntkd->nkgt', q_rot, k_cache, preferred_element_type=jnp.float32) * score_scale
    s_new = jnp.einsum('nkgd,nkd->nkg', q_rot, k_rot, preferred_element_type=jnp.float32) * score_scale
    s_cache = ATTN_CAP * jnp.tanh(s_cache / ATTN_CAP)
    s_new = ATTN_CAP * jnp.tanh(s_new / ATTN_CAP)
    valid_mask = jnp.arange(ctx_len)[None, :] < seq_lens[:, None]
    s_cache = jnp.where(valid_mask[:, None, None, :], s_cache, -1e30)
    row_max = jnp.maximum(jnp.max(s_cache, axis=-1), s_new)
    p_cache = jnp.exp(s_cache - row_max[..., None])
    p_new = jnp.exp(s_new - row_max)
    denominator = jnp.sum(p_cache, axis=-1) + p_new
    weighted = jnp.einsum('nkgt,ntkd->nkgd', p_cache.astype(jnp.bfloat16), v_cache, preferred_element_type=jnp.float32)
    weighted = weighted + p_new.astype(jnp.bfloat16).astype(jnp.float32)[..., None] * v_new.astype(jnp.float32)[:, :, None, :]
    return (weighted / denominator[..., None]).astype(jnp.bfloat16).reshape(tokens, kv_heads * group_size * head_dim)


def solution(mesh):
    tp_size = mesh.shape['t']
    in_specs = (P(), P(), P(), P(), P(None, 't'), P(None, 't'), P(None, 't'), P('t', None), P(), P(), P(None, 't'), P(None, 't'), P('t', None), P(), P(), P(None, None, 't', None), P(None, None, 't', None), P(('v', 't'), None))

    def local_step(hidden_in, seq_lens, target, g_attn_pre, w_q, w_k, w_v, w_o, g_attn_post, g_mlp_pre, w_gate, w_up, w_down, g_mlp_post, g_final, k_cache, v_cache, embed_table):
        normed = rms_norm(hidden_in, g_attn_pre).astype(jnp.bfloat16)
        attn_vec = attention(normed, seq_lens, w_q, w_k, w_v, k_cache, v_cache)
        attn_part = jnp.dot(attn_vec, w_o, preferred_element_type=jnp.float32)
        attn_out = lax.psum(attn_part, 't')
        hidden_mid = (hidden_in.astype(jnp.float32) + rms_norm(attn_out, g_attn_post)).astype(jnp.bfloat16)
        mlp_in = rms_norm(hidden_mid, g_mlp_pre).astype(jnp.bfloat16)
        gate_proj = jnp.dot(mlp_in, w_gate, preferred_element_type=jnp.float32)
        up_proj = jnp.dot(mlp_in, w_up, preferred_element_type=jnp.float32)
        activated = (jax.nn.gelu(gate_proj, approximate=True) * up_proj).astype(jnp.bfloat16)
        mlp_part = jnp.dot(activated, w_down, preferred_element_type=jnp.float32)
        mlp_out = lax.psum(mlp_part, 't')
        hidden_out = (hidden_mid.astype(jnp.float32) + rms_norm(mlp_out, g_mlp_post)).astype(jnp.bfloat16)
        final_h = rms_norm(hidden_out, g_final).astype(jnp.bfloat16)
        logits = lax.dot_general(final_h, embed_table, (((1,), (1,)), ((), ())), preferred_element_type=jnp.float32)
        capped = FINAL_CAP * jnp.tanh(logits / FINAL_CAP)
        vocab_local = embed_table.shape[0]
        shard_index = lax.axis_index('v') * tp_size + lax.axis_index('t')
        row_ids = shard_index * vocab_local + jnp.arange(vocab_local)
        local_max = jnp.max(capped, axis=1)
        local_sum = jnp.sum(jnp.exp(capped - local_max[:, None]), axis=1)
        local_tgt = jnp.sum(jnp.where(row_ids[None, :] == target[:, None], capped, 0.0), axis=1)
        gathered = lax.all_gather(jnp.stack([local_max, local_sum, local_tgt]), ('v', 't'))
        glob_max = jnp.max(gathered[:, 0], axis=0)
        glob_sum = jnp.sum(gathered[:, 1] * jnp.exp(gathered[:, 0] - glob_max[None, :]), axis=0)
        logprob = jnp.sum(gathered[:, 2], axis=0) - glob_max - jnp.log(glob_sum)
        return logprob, hidden_out

    return jax.shard_map(local_step, mesh=mesh, in_specs=in_specs, out_specs=(P(), P()), check_vma=False)
```

profile of v0, /device:TPU:0, one launch (start us, length us, event | category | flops | bytes accessed | tf_op | source)
XLA Modules:
  0.0 680.1 jit_solution(9327858685969552033)
XLA Ops:
  10.2 3.3 fusion.8
  13.5 5.7 fusion.80
  20.3 2.3 copy.46
  23.9 4.4 convolution_bitcast_fusion
  28.3 3.1 multiply_cosine_fusion.1
  31.4 2.3 fusion.68
  36.3 2.5 fusion.65
  39.8 3.1 multiply_reduce_fusion.2
  44.1 9.2 %fusion.85 = (f32[1024,2]{1,0:T(8,128)S(1)}, f32[1024,2,32]{2,1,0:T(2,128)}) fusion(bf16[1024,32,1,256]{3,1,2,0:T(8,128)(2,1)} %param.33, bf16[1024,2,128]{2,1,0:T(2,128)(2,1)} %copy-done.4, bf16[1024,2,128]{2,1,0:T(2,128)(2,1)} %copy-done.3, pred[1024,32]{1,0:T(8,128)(4,1)S(1)} %iota_compare_fusion), kind=kOutput, calls=%fused_computation.115 | convolution fusion | flops 35911680 | bytes 18128896 | tf_op jit(solution)/shard_map/nkgd,ntkd->nkgt/dot_general | solution.py:37
  53.8 15.5 %fusion.57 = f32[1024,2]{1,0:T(8,128)S(1)} fusion(f32[1024,2,32]{2,1,0:T(2,128)} %get-tuple-element.23, f32[1024,2]{1,0:T(8,128)S(1)} %copy.35), kind=kLoop, calls=%fused_computation.70 | loop fusion | flops 129024 | bytes 278528 | tf_op jit(solution)/shard_map/reduce_sum | solution.py:46
  70.8 4.3 fusion.39
  75.1 8.2 %fusion.34 = bf16[1024,2,256]{2,1,0:T(2,128)(2,1)S(1)} fusion(bf16[1024,32,1,256]{3,1,2,0:T(8,128)(2,1)} %param.34, f32[1024,2]{1,0:T(8,128)S(1)} %copy-done.6, f32[1024,256]{1,0:T(8,128)S(1)} %fusion.39, f32[1024,2]{1,0:T(8,128)S(1)} %copy.36, f32[1024,2,32]{2,1,0:T(2,128)S(1)} %copy-done.5, f32[1024,2]{1,0:T(8,128)S(1)} %copy.35), kind=kOutput, calls=%fused_computation.49 | convolution fusion | flops 35782656 | bytes 19161088 | tf_op jit(solution)/shard_map/nkgt,ntkd->nkgd/dot_general | solution.py:47
  83.5 5.1 fusion.86
  88.7 183.3 %all-reduce.3.cloned.1.call-done = f32[1024,2304]{1,0:T(8,128)} async-done(((f32[1024,2304]{1,0:T(8,128)}), f32[1024,2304]{1,0:T(8,128)}) %all-reduce.3.cloned.1.call-update) | async-done | bytes 9437200 | tf_op jit(solution)/shard_map/psum | solution.py:60
  272.0 4.4 multiply_reduce_fusion.1
  276.4 6.3 fusion.12
  284.9 15.7 %fusion.37 = f32[1024,2304]{1,0:T(8,128)} fusion(bf16[2304,2304]{1,0:T(8,128)(2,1)} %param.28, bf16[1024,2304]{1,0:T(8,128)(2,1)S(1)} %get-tuple-element.9, f32[2304]{0:T(1024)S(1)} %convert_add_fusion.4, f32[1024]{0:T(1024)S(1)} %add_rsqrt_fusion.2), kind=kOutput, calls=%fused_computation.51 | convolution fusion | flops 10881073152 | bytes 24785920 | tf_op jit(solution)/shard_map/dot_general | solution.py:63
  300.6 35.3 %fusion.25 = f32[1024,2304]{1,0:T(8,128)} fusion(bf16[2304,2304]{1,0:T(8,128)(2,1)} %param.30, f32[1024,2304]{1,0:T(8,128)} %fusion.37, bf16[2304,2304]{1,0:T(8,128)(2,1)} %param.29, bf16[1024,2304]{1,0:T(8,128)(2,1)} %copy-done.2, f32[2304]{0:T(1024)S(1)} %convert_add_fusion.4, f32[1024]{0:T(1024)S(1)} %add_rsqrt_fusion.2), kind=kOutput, calls=%fused_computation.39 | convolution fusion | flops 21776302080 | bytes 44839936 | tf_op jit(solution)/shard_map/dot_general | solution.py:66
  337.2 179.2 %all-reduce.5.cloned.1.call-done = f32[1024,2304]{1,0:T(8,128)} async-done(((f32[1024,2304]{1,0:T(8,128)}), f32[1024,2304]{1,0:T(8,128)}) %all-reduce.5.cloned.1.call-update) | async-done | bytes 9437200 | tf_op jit(solution)/shard_map/psum | solution.py:67
  516.4 4.4 multiply_reduce_fusion
  520.8 9.3 %fusion.5 = (f32[1024]{0:T(1024)S(1)}, bf16[1024,2304]{1,0:T(8,128)(2,1)}) fusion(f32[2304]{0:T(1024)S(1)} %convert_add_fusion.3, f32[1024,2304]{1,0:T(8,128)} %all-reduce.5.cloned.1.call-done, f32[1024]{0:T(1024)S(1)} %add_rsqrt_fusion.1, bf16[1024,2304]{1,0:T(8,128)(2,1)} %copy-done.2), kind=kLoop, calls=%fused_computation.17 | loop fusion | flops 18873344 | bytes 18891776 | tf_op jit(solution)/shard_map/reduce_sum | solution.py:14
  530.1 87.9 %fusion = (f32[1024]{0:T(1024)S(1)}, f32[1024,16000]{1,0:T(8,128)}) fusion(bf16[16000,2304]{1,0:T(8,128)(2,1)} %param.35, bf16[1024,2304]{1,0:T(8,128)(2,1)} %get-tuple-element.7, f32[2304]{0:T(1024)S(1)} %convert_add_fusion.2, f32[1024]{0:T(1024)S(1)} %add_rsqrt_fusion), kind=kOutput, calls=%fused_computation.3 | convolution fusion | flops 75556061184 | bytes 144000000 | tf_op jit(solution)/shard_map/dot_general | solution.py:70
  618.0 30.5 %exponential_reduce_fusion = (f32[1024]{0:T(1024)S(1)}, f32[1024]{0:T(1024)S(1)}) fusion(f32[1024,16000]{1,0:T(8,128)} %get-tuple-element.25, f32[1024]{0:T(1024)S(1)} %get-tuple-element.24, s32[1024]{0:T(1024)S(1)} %copy-done.15, s32[16000]{0:T(1024)S(1)} %copy-done.7), kind=kLoop, calls=%fused_computation.1 | loop fusion | flops 114685952 | bytes 65616384 | tf_op jit(solution)/shard_map/reduce_sum | solution.py:76
  648.6 23.4 %all-gather.1 = f32[16,3,1024]{2,1,0:T(4,128)S(1)} all-gather(f32[1,3,1024]{2,1,0:T(4,128)S(1)} %maximum_bitcast_fusion), channel_id=2, replica_groups=mesh['t'=4,'v'=4] {'v','t'}, dimensions={0}, use_global_device_ids=true | all-gather | bytes 208896 | tf_op jit(solution)/shard_map/all_gather | solution.py:78
  (69 shorter events, 16.8 us)
Async XLA Ops:
  7.2 76.4 %copy-start = (bf16[512,2304]{1,0:T(8,128)(2,1)S(1)}, bf16[512,2304]{1,0:T(8,128)(2,1)}, u32[]{:S(2)}) copy-start(bf16[512,2304]{1,0:T(8,128)(2,1)} %param.25) | copy-start | bytes 7077892
  7.2 264.8 %all-reduce.3.cloned.1.call-start = ((), (), s32[]{:S(2)}) async-start(), calls=%async_computation | async-start | bytes 18874368 | tf_op jit(solution)/shard_map/psum | solution.py:60
  10.2 13.8 %copy-start.8 = (f32[2304]{0:T(1024)}, f32[2304]{0:T(1024)S(1)}, u32[]{:S(2)}) copy-start(f32[2304]{0:T(1024)S(1)} %convert_add_fusion.6) | copy-start | bytes 27652
  13.5 5.7 copy-start.13
  23.9 4.4 copy-start.16
  38.8 0.8 copy-start.3
  38.8 1.0 copy-start.4
  44.1 26.7 %copy-start.14 = (f32[1024]{0:T(1024)S(1)}, f32[1024]{0:T(1024)}, u32[]{:S(2)}) copy-start(f32[1024]{0:T(1024)} %copy-done.13) | copy-start | bytes 12292
  70.8 4.3 copy-start.5
  70.8 4.3 copy-start.6
  83.5 5.2 copy-start.9
  83.5 5.2 copy-start.10
  88.6 427.8 %all-reduce.5.cloned.1.call-start = ((), (), s32[]{:S(2)}) async-start(), calls=%async_computation.1 | async-start | bytes 18874368 | tf_op jit(solution)/shard_map/psum | solution.py:67
  282.7 2.2 copy-start.2
  335.9 0.7 copy-start.11
  335.9 0.7 copy-start.12
  530.1 87.9 %copy-start.7 = (s32[16000]{0:T(1024)S(1)}, s32[16000]{0:T(1024)}, u32[]{:S(2)}) copy-start(s32[16000]{0:T(1024)} %iota_add_fusion) | copy-start | bytes 192004
  530.1 87.9 %copy-start.15 = (s32[1024]{0:T(1024)S(1)}, s32[1024]{0:T(1024)}, u32[]{:S(2)}) copy-start(s32[1024]{0:T(1024)} %param.20) | copy-start | bytes 12292
  618.0 54.8 %copy-start.1 = (bf16[512,2304]{1,0:T(8,128)(2,1)S(1)}, bf16[512,2304]{1,0:T(8,128)(2,1)}, u32[]{:S(2)}) copy-start(bf16[512,2304]{1,0:T(8,128)(2,1)} %param.25) | copy-start | bytes 7077892
Sparse Core Ops, SparseCore 0:
  88.8 183.2 all-reduce.2
  336.0 180.3 all-reduce.4
where the time goes:
time: 689 us; the launch traced here: 680 us
  waiting for transfers between devices  363 us (53%)
  matrix products  176 us (26%)
  other arithmetic  90.2 us (13%)
  blocking collectives  23.4 us (3%)
  between operations  14.8 us (2%)
  local copies, waits for them, and re-layouts  13.4 us (2%)
    psum x1, waiting for transfers between devices, local_step(): attn_out = lax.psum(attn_part, 't')  183 us
    psum x1, waiting for transfers between devices, local_step(): mlp_out = lax.psum(mlp_part, 't')  179 us
    dot_general x1, matrix products, local_step(): lax.dot_general(final_h, embed_table, (((1,), (1,)), ((), ())), preferred...  87.9 us
    dot_general x1, matrix products, local_step(): mlp_part = jnp.dot(activated, w_down, preferred_element_type=jnp.float32)  35.3 us
    reduce_sum x1, other arithmetic, local_step(): local_sum = jnp.sum(jnp.exp(capped - local_max[:, None]), axis=1)  30.5 us
    reduce_sum x5, other arithmetic, rms_norm(): jnp.mean(x_f32 * x_f32, axis=-1, keepdims=True) + NORM_EPS  27.7 us
    all_gather x1, blocking collectives, local_step(): lax.all_gather(jnp.stack([local_max, local_sum, local_tgt]), ('v', 't'))  23.4 us
    dot_general x1, matrix products, local_step(): gate_proj = jnp.dot(mlp_in, w_gate, preferred_element_type=jnp.float32)  15.7 us
  transfers between devices with their start and end apart: 2, of which 2 were waited for; matrix products, arithmetic and copies ran while one was open for 0% of the time, Pallas kernels for 0%

commit v1 on v0

v1 whole, which is shorter than its diff:
```python
import functools

import jax
import jax.numpy as jnp
from jax import lax
from jax.experimental import pallas as pl
from jax.experimental.pallas import tpu as pltpu
from jax.sharding import PartitionSpec as P

ATTN_CAP = 50.0
FINAL_CAP = 30.0
NORM_EPS = 1e-6
ROPE_BASE = 10000.0
MESH = pl.DeviceIdType.MESH
F32 = jnp.float32
BF16 = jnp.bfloat16

CHUNKS = 2
E_ROWS = 800
E_SLOTS = 4


def flip_t(t, mask):
    if mask == 0:
        return t
    if mask == 1:
        return t + 1 - 2 * (t % 2)
    if mask == 2:
        return (t + 2) % 4
    return 3 - t


def flip_v(v, mask):
    return flip_t(v, mask)


def rms(values, gain):
    return values * lax.rsqrt(jnp.mean(values * values, axis=-1, keepdims=True) + NORM_EPS) * gain


def layer_kernel(x_hbm, seq_ref, cos_ref, sin_ref, gain_ref, wq_hbm, wk_hbm, wv_hbm, wo_hbm, wg_hbm, wu_hbm, wd_hbm, k_hbm, v_hbm, y_ref,
                 xbuf, wq, wk, wv, wo, wg, wu, wd, kbuf, vbuf, sbuf, part, red1, red2, mbuf, mid, act, x_sem, w_sem, kv_sem, send_sem, recv_sem):
    t = lax.axis_index('t')
    v = lax.axis_index('v')
    tp, piece = 4, y_ref.shape[1]
    rows = tp * piece
    block = CHUNKS * piece
    width = x_hbm.shape[1]
    half = width // 2
    head = wk.shape[1]
    ctx = kbuf.shape[0] // rows
    score_scale = head ** -0.5

    def token0(c, o):
        return tp * block * v + block * o + piece * c

    x_copies = []
    for c in range(CHUNKS):
        for o in range(tp):
            x_copies.append(pltpu.make_async_copy(x_hbm.at[pl.ds(pl.multiple_of(token0(c, o), piece), piece)], xbuf.at[c, pl.ds(o * piece, piece)], x_sem.at[c, o]))

    def kv_copies(c):
        out = []
        for o in range(tp):
            src = pl.ds(pl.multiple_of(token0(c, o) * ctx, piece * ctx), piece * ctx)
            dst = pl.ds(o * piece * ctx, piece * ctx)
            out.append(pltpu.make_async_copy(k_hbm.at[src], kbuf.at[dst], kv_sem.at[c, 0, o]))
            out.append(pltpu.make_async_copy(v_hbm.at[src], vbuf.at[dst], kv_sem.at[c, 1, o]))
        return out

    pairs = ((wq_hbm, wq), (wk_hbm, wk), (wv_hbm, wv), (wo_hbm, wo), (wg_hbm, wg), (wu_hbm, wu), (wd_hbm, wd))
    w_copies = [pltpu.make_async_copy(src, dst, w_sem.at[i]) for i, (src, dst) in enumerate(pairs)]
    for cp in x_copies[:tp]:
        cp.start()
    for cp in w_copies[:3]:
        cp.start()
    for cp in kv_copies(0):
        cp.start()
    w_copies[3].start()
    for cp in x_copies[tp:]:
        cp.start()
    for cp in w_copies[4:]:
        cp.start()

    barrier = pltpu.get_barrier_semaphore()
    for mask in (1, 2):
        pl.semaphore_signal(barrier, inc=1, device_id=(flip_t(t, mask), v), device_id_type=MESH)

    def attend(c):
        for cp in x_copies[c * tp:(c + 1) * tp]:
            cp.wait()
        a = rms(xbuf[c].astype(F32), gain_ref[0:1, :]).astype(BF16)
        if c == 0:
            for cp in w_copies[:3]:
                cp.wait()
        q = jnp.dot(a, wq[...], preferred_element_type=F32)
        k = jnp.dot(a, wk[...], preferred_element_type=F32)
        val = jnp.dot(a, wv[...], preferred_element_type=F32).astype(BF16).astype(F32)
        cos_t = cos_ref[c * rows:(c + 1) * rows, :]
        sin_t = sin_ref[c * rows:(c + 1) * rows, :]

        def rope(z):
            low, high = z[:, :head // 2], z[:, head // 2:]
            return jnp.concatenate([low * cos_t - high * sin_t, high * cos_t + low * sin_t], axis=1).astype(BF16).astype(F32)

        q0, q1, k = rope(q[:, :head]), rope(q[:, head:]), rope(k)
        groups = rows // 8

        def by_group(first, second):
            return jnp.concatenate([piece8 for g in range(groups) for piece8 in (first[8 * g:8 * g + 8], second[8 * g:8 * g + 8])], axis=0)

        q_all = by_group(q0, q1)
        s_new = jnp.sum(q_all * by_group(k, k), axis=1, keepdims=True)
        val_all = by_group(val, val)
        q_bf = q_all.astype(BF16)
        for cp in kv_copies(c):
            cp.wait()
        for g in range(groups):
            sbuf[16 * g:16 * g + 16, :] = lax.dot_general(q_bf[16 * g:16 * g + 16], kbuf[8 * ctx * g:8 * ctx * (g + 1), :], (((1,), (1,)), ((), ())), preferred_element_type=F32)
        seq8 = seq_ref[c * rows:(c + 1) * rows, :]
        seq_all = by_group(seq8, seq8)
        seq_all = jnp.concatenate([seq_all] * (8 * ctx // 128), axis=1)
        lane = lax.broadcasted_iota(jnp.int32, (2 * rows, 8 * ctx), 1)
        row = lax.broadcasted_iota(jnp.int32, (2 * rows, 8 * ctx), 0)
        valid = jnp.logical_and(lane // ctx == row % 8, lane % ctx < seq_all)
        s = ATTN_CAP * jnp.tanh(sbuf[...] * (score_scale / ATTN_CAP))
        s_new = ATTN_CAP * jnp.tanh(s_new * (score_scale / ATTN_CAP))
        s = jnp.where(valid, s, -1e30)
        top = jnp.maximum(jnp.max(s, axis=1, keepdims=True), s_new)
        p = jnp.where(valid, jnp.exp(s - top), 0.0)
        p_new = jnp.exp(s_new - top)
        denom = jnp.sum(p, axis=1, keepdims=True) + p_new
        p_bf = p.astype(BF16)
        for g in range(groups):
            sbuf[16 * g:16 * g + 16, :head] = jnp.dot(p_bf[16 * g:16 * g + 16], vbuf[8 * ctx * g:8 * ctx * (g + 1), :], preferred_element_type=F32)
        o_all = (sbuf[:, :head] + p_new.astype(BF16).astype(F32) * val_all) / denom
        o0 = jnp.concatenate([o_all[16 * g:16 * g + 8] for g in range(groups)], axis=0)
        o1 = jnp.concatenate([o_all[16 * g + 8:16 * g + 16] for g in range(groups)], axis=0)
        if c + 1 < CHUNKS:
            for cp in kv_copies(c + 1):
                cp.start()
        if c == 0:
            w_copies[3].wait()
        o = jnp.concatenate([o0, o1], axis=1).astype(BF16)
        part[c] = jnp.dot(o, wo[...], preferred_element_type=F32)

    order = ((2, 1), (1, 2))

    def cols(h):
        return pl.ds(h * half, half)

    def rows_of(o):
        return pl.ds(pl.multiple_of(o * piece, piece), piece)

    def remote(src, dst, c, phase, h, i, mask):
        return pltpu.make_async_remote_copy(src_ref=src, dst_ref=dst, send_sem=send_sem.at[c, phase, h, i], recv_sem=recv_sem.at[c, phase, h, i],
                                            device_id=(flip_t(t, mask), v), device_id_type=MESH)

    def scatter1(c, phase, h, i):
        m1, m2 = order[h]
        owner = flip_t(t, 3) if i else flip_t(t, m1)
        return remote(part.at[c, rows_of(owner), cols(h)], red1.at[phase // 2, c, h, i], c, phase, h, i, m1)

    def scatter2(c, phase, h):
        return remote(red1.at[phase // 2, c, h, 1], red2.at[phase // 2, c, h], c, phase, h, 2, order[h][1])

    def scatter_start(c, phase):
        for i in (1, 0):
            for h in range(2):
                scatter1(c, phase, h, i).start()

    def scatter_pass(c, phase):
        for h in range(2):
            scatter1(c, phase, h, 1).wait_recv()
            red1[phase // 2, c, h, 1] = red1[phase // 2, c, h, 1] + part[c, rows_of(flip_t(t, order[h][1])), h * half:(h + 1) * half]
            scatter2(c, phase, h).start()

    def scatter_end(c, phase):
        got = []
        for h in range(2):
            scatter1(c, phase, h, 0).wait_recv()
            scatter2(c, phase, h).wait_recv()
            got.append(part[c, rows_of(t), h * half:(h + 1) * half] + red1[phase // 2, c, h, 0] + red2[phase // 2, c, h])
        for h in range(2):
            scatter1(c, phase, h, 0).wait_send()
            scatter1(c, phase, h, 1).wait_send()
            scatter2(c, phase, h).wait_send()
        return jnp.concatenate(got, axis=1)

    def gather(c, h, i):
        m1, m2 = order[h]
        where = mbuf.at[c, rows_of(flip_t(t, m2) if i == 2 else t), cols(h)]
        return remote(where, where, c, 1, h, i, m1 if i else m2)

    def gather_start(c):
        for i in (0, 1):
            for h in range(2):
                gather(c, h, i).start()

    def gather_pass(c):
        for h in range(2):
            gather(c, h, 0).wait_recv()
            gather(c, h, 2).start()

    def gather_end(c):
        for h in range(2):
            gather(c, h, 1).wait_recv()
            gather(c, h, 2).wait_recv()

    def gather_sent(c):
        for h in range(2):
            for i in range(3):
                gather(c, h, i).wait_send()

    def middle(c):
        attn_out = scatter_end(c, 0)
        x_own = xbuf[c, rows_of(t), :].astype(F32)
        x1 = (x_own + rms(attn_out, gain_ref[1:2, :])).astype(BF16).astype(F32)
        mid[c] = x1
        mbuf[c, rows_of(t), :] = rms(x1, gain_ref[2:3, :]).astype(BF16).astype(F32)

    def mlp(c):
        if c == 0:
            for cp in w_copies[4:]:
                cp.wait()
        m = mbuf[c].astype(BF16)
        tiles = 3
        wide = width // tiles

        def up_tile(i, carry):
            at = pl.ds(pl.multiple_of(i * wide, 128), wide)
            gate = jnp.dot(m, wg[:, at], preferred_element_type=F32)
            up = jnp.dot(m, wu[:, at], preferred_element_type=F32)
            act[:, at] = (jax.nn.gelu(gate, approximate=True) * up).astype(BF16)
            return carry

        lax.fori_loop(0, tiles, up_tile, 0)

        def down_tile(i, carry):
            at = pl.ds(pl.multiple_of(i * wide, 128), wide)
            part[c, :, at] = jnp.dot(act[...], wd[:, at], preferred_element_type=F32)
            return carry

        lax.fori_loop(0, tiles, down_tile, 0)

    attend(0)
    pl.semaphore_wait(barrier, 2)
    scatter_start(0, 0)
    attend(1)
    scatter_start(1, 0)
    scatter_pass(0, 0)
    scatter_pass(1, 0)
    middle(0)
    gather_start(0)
    middle(1)
    gather_start(1)
    gather_pass(0)
    gather_end(0)
    gather_pass(1)
    mlp(0)
    scatter_start(0, 2)
    gather_end(1)
    mlp(1)
    scatter_start(1, 2)
    scatter_pass(0, 2)
    scatter_pass(1, 2)
    for c in range(CHUNKS):
        y_ref[c] = (mid[c] + rms(scatter_end(c, 2), gain_ref[3:4, :])).astype(BF16).astype(F32)
        gather_sent(c)


def layer(tokens, x, seq_rows, cos_t, sin_t, gains, w_q, w_k, w_v, w_o, w_gate, w_up, w_down, k_rows, v_rows):
    width = x.shape[1]
    piece = tokens // 16 // CHUNKS
    rows = 4 * piece
    head = w_k.shape[1]
    ctx = k_rows.shape[0] // tokens
    ff = w_gate.shape[1]
    vm = pl.BlockSpec(memory_space=pltpu.VMEM)
    hbm = pl.BlockSpec(memory_space=pl.ANY)
    return pl.pallas_call(
        layer_kernel,
        out_shape=jax.ShapeDtypeStruct((CHUNKS, piece, width), F32),
        in_specs=[hbm] + [vm] * 4 + [hbm] * 9,
        out_specs=vm,
        scratch_shapes=[
            pltpu.VMEM((CHUNKS, rows, width), BF16),
            *[pltpu.VMEM(w.shape, BF16) for w in (w_q, w_k, w_v, w_o, w_gate, w_up, w_down)],
            pltpu.VMEM((rows * ctx, head), BF16),
            pltpu.VMEM((rows * ctx, head), BF16),
            pltpu.VMEM((2 * rows, 8 * ctx), F32),
            pltpu.VMEM((CHUNKS, rows, width), F32),
            pltpu.VMEM((2, CHUNKS, 2, 2, piece, width // 2), F32),
            pltpu.VMEM((2, CHUNKS, 2, piece, width // 2), F32),
            pltpu.VMEM((CHUNKS, rows, width), F32),
            pltpu.VMEM((CHUNKS, piece, width), F32),
            pltpu.VMEM((rows, ff), BF16),
            pltpu.SemaphoreType.DMA((CHUNKS, 4)),
            pltpu.SemaphoreType.DMA((7,)),
            pltpu.SemaphoreType.DMA((CHUNKS, 2, 4)),
            pltpu.SemaphoreType.DMA((CHUNKS, 3, 2, 3)),
            pltpu.SemaphoreType.DMA((CHUNKS, 3, 2, 3)),
        ],
        compiler_params=pltpu.CompilerParams(collective_id=0, has_side_effects=True, vmem_limit_bytes=66_000_000),
        name='layer',
    )(x, seq_rows, cos_t, sin_t, gains, w_q, w_k, w_v, w_o, w_gate, w_up, w_down, k_rows, v_rows)


AXES = ('x', 'z', 'y')
FLIP = {'x': (0, 2), 'y': (1, 0), 'z': (2, 0), 'c': (0, 1)}


def head_kernel(y_own, gain_ref, tgt_ref, e_hbm, logp_ref, y_hbm,
                ybuf, hbuf, ystage, ebuf, lg0, lg1, stat, stats, e_sem, y_sem, send_sem, recv_sem, stat_send, stat_recv):
    t = lax.axis_index('t')
    v = lax.axis_index('v')
    me = 4 * v + t
    piece, width = y_own.shape[1:]
    toks = 16 * piece
    third = width // 3
    sub = E_ROWS // 2
    vocab_local = e_hbm.shape[0]
    tiles = vocab_local // E_ROWS
    total = tiles * CHUNKS

    barrier = pltpu.get_barrier_semaphore()
    for j in range(1, 16):
        other = (me + j) % 16
        pl.semaphore_signal(barrier, inc=1, device_id=(other % 4, other // 4), device_id_type=MESH)

    def e_copy(i):
        tile = i % tiles
        slot = i % E_SLOTS
        return pltpu.make_async_copy(e_hbm.at[pl.ds(pl.multiple_of(tile * E_ROWS, E_ROWS), E_ROWS)], ebuf.at[slot], e_sem.at[slot])

    for i in range(E_SLOTS - 1):
        e_copy(i).start()
    for c in range(CHUNKS):
        ybuf[c, pl.ds(pl.multiple_of(me * piece, piece), piece), :] = y_own[c]
    lg1[...] = jnp.zeros_like(lg1)
    pl.semaphore_wait(barrier, 15)

    def axes_of(p, bits):
        order = [AXES[(p + s) % 3] for s in range(3)]
        mt = mv = 0
        for s in range(3):
            if bits >> s & 1:
                mt ^= FLIP[order[s]][0]
                mv ^= FLIP[order[s]][1]
        return mt, mv

    def block_copy(c, p, s, bits):
        mt, mv = axes_of(p, bits)
        blk = 4 * flip_v(v, mv) + flip_t(t, mt)
        at = ybuf.at[c, pl.ds(pl.multiple_of(blk * piece, piece), piece), pl.ds(p * third, third)]
        src = y_own.at[c, :, pl.ds(p * third, third)] if bits == 0 else at
        ft, fv = FLIP['c'] if s == 3 else FLIP[AXES[(p + s) % 3]]
        i = 2 ** s - 1 + bits
        return pltpu.make_async_remote_copy(src_ref=src, dst_ref=at, send_sem=send_sem.at[c, p, i], recv_sem=recv_sem.at[c, p, i],
                                            device_id=(flip_t(t, ft), flip_v(v, fv)), device_id_type=MESH)

    def spread(c, step):
        if step == 0:
            for s in (0, 1, 2, 3):
                for p in range(3):
                    block_copy(c, p, s, 0).start()
        elif step <= 3:
            s = step - 1
            for bits in range(2 ** s):
                for p in range(3):
                    block_copy(c, p, s, bits).wait_recv()
                    for later in range(s + 1, 4):
                        block_copy(c, p, later, bits | 1 << s).start()
        else:
            for p in range(3):
                for bits in range(8):
                    block_copy(c, p, 3, bits).wait_recv()

    def spread_sent(c):
        for p in range(3):
            for s in range(4):
                for bits in range(2 ** s):
                    block_copy(c, p, s, bits).wait_send()

    def y_copy(c, b):
        return pltpu.make_async_copy(ystage.at[pl.ds(b * piece, piece)], y_hbm.at[pl.ds((b * CHUNKS + c) * piece, piece)], y_sem.at[c, b])

    def stat_copy(c, j):
        other = (me + j) % 16
        return pltpu.make_async_remote_copy(src_ref=stat.at[c], dst_ref=stats.at[c, me], send_sem=stat_send.at[c, j - 1], recv_sem=stat_recv.at[c, j - 1],
                                            device_id=(other % 4, other // 4), device_id_type=MESH)

    for step in range(5):
        spread(0, step)

    lanes = lax.broadcasted_iota(jnp.int32, (8, toks), 0)

    def reduce_rows(lg, first_row, tgt):
        rel = tgt - first_row
        s_acc = [jnp.zeros((8, toks), F32) for _ in range(2)]
        t_acc = [jnp.zeros((8, toks), F32) for _ in range(2)]
        for r in range(sub // 8):
            th = jnp.tanh(lg[8 * r:8 * r + 8, :] * (1.0 / FINAL_CAP))
            s_acc[r % 2] = s_acc[r % 2] + jnp.exp(th * FINAL_CAP)
            t_acc[r % 2] = t_acc[r % 2] + jnp.where(lanes == rel - 8 * r, th, 0.0)
        return s_acc[0] + s_acc[1], t_acc[0] + t_acc[1]

    for c in range(CHUNKS):
        strip = 128
        if c:
            for b in range(16):
                y_copy(c - 1, b).wait()
        for r in range(toks // strip):
            yv = ybuf[c, r * strip:(r + 1) * strip, :]
            ystage[r * strip:(r + 1) * strip, :] = yv.astype(BF16)
            hbuf[:, r * strip:(r + 1) * strip] = rms(yv, gain_ref[4:5, :]).T.astype(BF16)
        for b in range(16):
            y_copy(c, b).start()
        tgt = jnp.broadcast_to(tgt_ref[c], (8, toks)) - me * vocab_local
        if c + 1 < CHUNKS:
            spread(c + 1, 0)

        def step(i, carry):
            s_sum, t_sum = carry
            n = c * tiles + i

            @pl.when(n + E_SLOTS - 1 < total)
            def _():
                e_copy(n + E_SLOTS - 1).start()

            e_copy(n).wait()
            slot = n % E_SLOTS
            lg0[...] = jnp.dot(ebuf[slot, :sub, :], hbuf[...], preferred_element_type=F32)
            s_part, t_part = reduce_rows(lg1, i * E_ROWS - sub, tgt)
            keep = i > 0
            s_sum = s_sum + jnp.where(keep, s_part, 0.0)
            t_sum = t_sum + jnp.where(keep, t_part, 0.0)
            lg1[...] = jnp.dot(ebuf[slot, sub:, :], hbuf[...], preferred_element_type=F32)
            s_part, t_part = reduce_rows(lg0, i * E_ROWS, tgt)
            if c + 1 < CHUNKS:
                for stage, at in ((1, 3), (2, 6), (3, 10), (4, 13)):
                    @pl.when(i == at)
                    def _(stage=stage):
                        spread(c + 1, stage)
            return s_sum + s_part, t_sum + t_part

        zero = jnp.zeros((8, toks), F32)
        s_sum, t_sum = lax.fori_loop(0, tiles, step, (zero, zero))
        s_part, t_part = reduce_rows(lg1, tiles * E_ROWS - sub, tgt)
        s_sum = jnp.sum(s_sum + s_part, axis=0, keepdims=True)
        t_sum = jnp.sum(t_sum + t_part, axis=0, keepdims=True)
        both = jnp.where(lanes == 0, s_sum, jnp.where(lanes == 1, t_sum, 0.0))
        stat[c] = both
        stats[c, me] = both
        for j in range(1, 16):
            stat_copy(c, j).start()

    for c in range(CHUNKS):
        for j in range(1, 16):
            stat_copy(c, j).wait_recv()
        tot = stats[c, 0]
        for b in range(1, 16):
            tot = tot + stats[c, b]
        logp_ref[c] = FINAL_CAP * tot[1:2, :] - jnp.log(tot[0:1, :])
    for c in range(CHUNKS):
        spread_sent(c)
        for j in range(1, 16):
            stat_copy(c, j).wait_send()
    for b in range(16):
        y_copy(CHUNKS - 1, b).wait()


def head(tokens, y_own, gains, tgt, table):
    piece, width = y_own.shape[1:]
    toks = 16 * piece
    vm = pl.BlockSpec(memory_space=pltpu.VMEM)
    hbm = pl.BlockSpec(memory_space=pl.ANY)
    return pl.pallas_call(
        head_kernel,
        out_shape=(jax.ShapeDtypeStruct((CHUNKS, 1, toks), F32), jax.ShapeDtypeStruct((tokens, width), BF16)),
        in_specs=[vm, vm, vm, hbm],
        out_specs=(vm, hbm),
        scratch_shapes=[
            pltpu.VMEM((CHUNKS, toks, width), F32),
            pltpu.VMEM((width, toks), BF16),
            pltpu.VMEM((toks, width), BF16),
            pltpu.VMEM((E_SLOTS, E_ROWS, width), BF16),
            pltpu.VMEM((E_ROWS // 2, toks), F32),
            pltpu.VMEM((E_ROWS // 2, toks), F32),
            pltpu.VMEM((CHUNKS, 8, toks), F32),
            pltpu.VMEM((CHUNKS, 16, 8, toks), F32),
            pltpu.SemaphoreType.DMA((E_SLOTS,)),
            pltpu.SemaphoreType.DMA((CHUNKS, 16)),
            pltpu.SemaphoreType.DMA((CHUNKS, 3, 15)),
            pltpu.SemaphoreType.DMA((CHUNKS, 3, 15)),
            pltpu.SemaphoreType.DMA((CHUNKS, 15)),
            pltpu.SemaphoreType.DMA((CHUNKS, 15)),
        ],
        compiler_params=pltpu.CompilerParams(collective_id=1, has_side_effects=True, vmem_limit_bytes=60_000_000),
        name='head',
    )(y_own, gains, tgt, table)


def solution(mesh):
    in_specs = (P(), P(), P(), P(), P(None, 't'), P(None, 't'), P(None, 't'), P('t', None), P(), P(), P(None, 't'), P(None, 't'), P('t', None), P(), P(), P(None, None, 't', None), P(None, None, 't', None), P(('v', 't'), None))

    def local_step(hidden_in, seq_lens, target, g_attn_pre, w_q, w_k, w_v, w_o, g_attn_post, g_mlp_pre, w_gate, w_up, w_down, g_mlp_post, g_final, k_cache, v_cache, embed_table):
        tokens = hidden_in.shape[0]
        group = tokens // 4
        piece = tokens // 16 // CHUNKS
        ctx, _, head_dim = k_cache.shape[1:]
        half_dim = head_dim // 2
        gains = 1.0 + jnp.stack([g_attn_pre, g_attn_post, g_mlp_pre, g_mlp_post, g_final]).astype(F32)
        seq = lax.dynamic_slice(seq_lens, (lax.axis_index('v') * group,), (group,))
        seq = seq.reshape(4, CHUNKS, piece).transpose(1, 0, 2).reshape(group)
        inv_freq = ROPE_BASE ** (-2.0 * jnp.arange(half_dim, dtype=F32) / head_dim)
        angles = seq.astype(F32)[:, None] * inv_freq[None, :]
        seq_rows = jnp.broadcast_to(seq[:, None], (group, 128))
        k_rows = k_cache.reshape(tokens * ctx, head_dim)
        v_rows = v_cache.reshape(tokens * ctx, head_dim)
        y_own = layer(tokens, hidden_in, seq_rows, jnp.cos(angles), jnp.sin(angles), gains, w_q, w_k, w_v, w_o, w_gate, w_up, w_down, k_rows, v_rows)
        tgt = target.reshape(16, CHUNKS, piece).transpose(1, 0, 2).reshape(CHUNKS, 1, 16 * piece)
        logp, hidden_out = head(tokens, y_own, gains, tgt, embed_table)
        logprob = logp.reshape(CHUNKS, 16, piece).transpose(1, 0, 2).reshape(tokens)
        return logprob, hidden_out

    return jax.shard_map(local_step, mesh=mesh, in_specs=in_specs, out_specs=(P(), P()), check_vma=False)
```

time: 689 us -> 218 us (0.32); the launches traced: 680 us -> 218 us
  waiting for transfers between devices: 363 us -> 0 us
  Pallas kernels: 0 us -> 202 us
  matrix products: 176 us -> 0 us
  other arithmetic: 90.2 us -> 2.57 us
  blocking collectives: 23.4 us -> 0 us
  between operations: 14.8 us -> 0.67 us
    psum x2 -> x0, waiting for transfers between devices: 363 us -> none  [the longest x1 183 us: local_step(): attn_out = lax.psum(attn_part, 't')]
    pallas_call x0 -> x2, Pallas kernels: none -> 202 us  [the longest x1 124 us: head(): pl.pallas_call(head_kernel, out_shape=(jax.ShapeDtypeStruct((CHUNKS, 1, t...]
    dot_general x9 -> x0, matrix products: 176 us -> none  [the longest x1 87.9 us: local_step(): lax.dot_general(final_h, embed_table, (((1,), (1,)), ((), ())), preferred...]
    reduce_sum x9 -> x0, other arithmetic: 73.9 us -> none  [the longest x1 30.5 us: local_step(): local_sum = jnp.sum(jnp.exp(capped - local_max[:, None]), axis=1)]
    all_gather x1 -> x0, blocking collectives: 23.4 us -> none  [local_step(): lax.all_gather(jnp.stack([local_max, local_sum, local_tgt]), ('v', 't'))]
  transfers between devices with their start and end apart: 2 -> 0, of which waited for: 2 -> 0; matrix products, arithmetic and copies ran while one was open for 0% -> 0% of each run, Pallas kernels for 0% -> 0%
where the time goes in v1:
time: 218 us
  Pallas kernels  202 us (93%)
  local copies, waits for them, and re-layouts  12.3 us (6%)
  other arithmetic  2.57 us (1%)
    pallas_call x1, Pallas kernels, head(): pl.pallas_call(head_kernel, out_shape=(jax.ShapeDtypeStruct((CHUNKS, 1, t...  124 us
    pallas_call x1, Pallas kernels, layer(): pl.pallas_call(layer_kernel, out_shape=jax.ShapeDtypeStruct((CHUNKS, piec...  78 us
    unnamed x1, local copies, waits for them, and re-layouts  4.82 us

profile of v1, /device:TPU:0, one launch (start us, length us, event | category | flops | bytes accessed | tf_op | source)
XLA Modules:
  0.0 217.8 jit_solution(1782258362105262856)
XLA Ops:
  0.6 0.8 dynamic_slice.3
  1.4 0.1 reshape.37
  1.5 0.1 broadcast_in_dim.4
  1.6 0.7 stack.18
  2.3 0.7 stack.19
  3.0 0.7 stack.20
  3.7 0.7 stack.21
  4.4 0.7 stack.22
  5.1 0.1 stack.23
  5.2 0.8 reshape.40
  5.9 0.7 reshape.41.tgt_ref
  6.6 0.6 convert_add_fusion.gain_ref
  7.2 0.8 broadcast_in_dim.10.seq_ref
  8.0 1.2 multiply_sine_fusion
  9.2 78.0 %layer.1.y_own = f32[2,32,2304]{2,1,0:T(8,128)} custom-call(bf16[1024,2304]{1,0:T(8,128)(2,1)} %x_hbm.1, s32[256,128]{1,0:T(8,128)} %broadcast_in_dim.10.seq_ref, f32[256,128]{1,0:T(8,128)} %get-tuple-element.7.cos_ref, f32[256,128]{1,0:T(8,128)} %get-tuple-element.6.sin_ref, f32[5,2304]{1,0:T(8,128)} %convert_add_fusion.gain_ref, bf16[2304,512]{1,0:T(8,128)(2,1)} %wq_hbm.1, ...), custom_call_target="tpu_custom_call" | custom-call | tf_op jit(solution)/shard_map/layer/pallas_call | solution.py:281
  87.2 124.2 %head.1 = (f32[2,1,512]{2,1,0:T(1,128)}, bf16[1024,2304]{1,0:T(8,128)(2,1)}) custom-call(f32[2,32,2304]{2,1,0:T(8,128)} %layer.1.y_own, f32[5,2304]{1,0:T(8,128)} %convert_add_fusion.gain_ref, s32[2,1,512]{2,1,0:T(1,128)} %reshape.41.tgt_ref, bf16[16000,2304]{1,0:T(8,128)(2,1)} %e_hbm.1), custom_call_target="tpu_custom_call" | custom-call | tf_op jit(solution)/shard_map/head/pallas_call | solution.py:478
  211.5 0.7 reduce
  212.2 0.1 reshape.42
  212.3 0.7 reshape.43
  212.9 4.8 %copy.28 = bf16[1024,2304]{1,0:T(8,128)(2,1)} copy(bf16[1024,2304]{1,0:T(8,128)(2,1)} %get-tuple-element.11) | data formatting | bytes 9437184
  (5 shorter events, 0.0 us)

commit v2 on v1

v2 whole, which is shorter than its diff:
```python
import jax
import jax.numpy as jnp
import numpy as np
from jax import lax
from jax.experimental import pallas as pl
from jax.experimental.pallas import tpu as pltpu
from jax.sharding import PartitionSpec as P

ATTN_CAP = 50.0
FINAL_CAP = 30.0
NORM_EPS = 1e-6
ROPE_BASE = 10000.0
MESH = pl.DeviceIdType.MESH
F32 = jnp.float32
BF16 = jnp.bfloat16

PIECES = (32, 32)
E_ROWS = 800
E_SLOTS = 8
AXES = ('x', 'z', 'y')
FLIP = {'x': (0, 2), 'y': (1, 0), 'z': (2, 0), 'c': (0, 1)}


def flip_t(t, mask):
    if mask == 0:
        return t
    if mask == 1:
        return t + 1 - 2 * (t % 2)
    if mask == 2:
        return (t + 2) % 4
    return 3 - t


def flip_v(v, mask):
    return flip_t(v, mask)


def rms(values, gain):
    return values * lax.rsqrt(jnp.mean(values * values, axis=-1, keepdims=True) + NORM_EPS) * gain


def kernel(x_hbm, seq_ref, tgt_ref, freq_ref, g_attn_pre, g_attn_post, g_mlp_pre, g_mlp_post, g_final,
           wq_hbm, wk_hbm, wv_hbm, wo_hbm, wg_hbm, wu_hbm, wd_hbm, k_hbm, v_hbm, e_hbm, logp_ref, y_hbm,
           xbuf, wq, wk, wv, wo, big, sbuf, part, red1, red2, ybuf, mid, act, lg0, lg1, stat, stats,
           x_sem, w_sem, kv_sem, e_sem, y_sem, send_sem, recv_sem, spread_send, spread_recv, stat_send, stat_recv):
    t = lax.axis_index('t')
    v = lax.axis_index('v')
    me = 4 * v + t
    chunks = len(PIECES)
    bases = [16 * sum(PIECES[:c]) for c in range(chunks)]
    width = x_hbm.shape[1]
    half, third = width // 2, width // 3
    ff = wg_hbm.shape[1]
    head = wk.shape[1]
    ctx = k_hbm.shape[0] // x_hbm.shape[0]
    score_scale = head ** -0.5
    groups_of = [4 * n for n in PIECES]
    toks_of = [16 * n for n in PIECES]

    def gain(ref):
        return 1.0 + ref[...].astype(F32).reshape(1, width)

    def group_rows(c):
        return pl.multiple_of(bases[c] + groups_of[c] * v, 8)

    x_copies = [pltpu.make_async_copy(x_hbm.at[pl.ds(group_rows(c), groups_of[c])], xbuf.at[c, pl.ds(0, groups_of[c])], x_sem.at[c]) for c in range(chunks)]

    def kv_at(c, i):
        return pl.ds(ff, groups_of[c] * ctx), pl.ds((2 * c + i) * head, head)

    def kv_copies(c):
        rows = pl.ds(pl.multiple_of(group_rows(c) * ctx, 8 * ctx), groups_of[c] * ctx)
        return [pltpu.make_async_copy(src.at[rows], big.at[kv_at(c, i)], kv_sem.at[c, i]) for i, src in enumerate((k_hbm, v_hbm))]

    pairs = ((wq_hbm, wq), (wk_hbm, wk), (wv_hbm, wv), (wo_hbm, wo), (wg_hbm, big.at[pl.ds(0, width)]), (wu_hbm, big.at[pl.ds(width, width)]), (wd_hbm, big.at[pl.ds(2 * width, ff)]))
    w_copies = [pltpu.make_async_copy(src, dst, w_sem.at[i]) for i, (src, dst) in enumerate(pairs)]
    x_copies[0].start()
    for cp in w_copies[:3]:
        cp.start()
    for cp in kv_copies(0):
        cp.start()
    w_copies[3].start()
    for c in range(1, chunks):
        x_copies[c].start()
        for cp in kv_copies(c):
            cp.start()
    w_copies[4].start()

    barrier = pltpu.get_barrier_semaphore()
    for j in range(1, 16):
        other = (me + j) % 16
        pl.semaphore_signal(barrier, inc=1, device_id=(other % 4, other // 4), device_id_type=MESH)

    def attend(c):
        rows = groups_of[c]
        x_copies[c].wait()
        a = rms(xbuf[c, :rows, :].astype(F32), gain(g_attn_pre)).astype(BF16)
        if c == 0:
            for cp in w_copies[:3]:
                cp.wait()
        q = jnp.dot(a, wq[...], preferred_element_type=F32)
        k = jnp.dot(a, wk[...], preferred_element_type=F32)
        val = jnp.dot(a, wv[...], preferred_element_type=F32).astype(BF16).astype(F32)
        start = group_rows(c)
        seq_row = seq_ref[pl.ds(start // 128, 1), :]
        lane = lax.broadcasted_iota(jnp.int32, (rows, 128), 1)
        row = lax.broadcasted_iota(jnp.int32, (rows, 128), 0)
        pos = jnp.sum(jnp.where(lane == row + start % 128, seq_row.astype(F32), 0.0), axis=1, keepdims=True)
        angle = pos * freq_ref[...]
        cos_t, sin_t = jnp.cos(angle), jnp.sin(angle)

        def rope(z):
            low, high = z[:, :head // 2], z[:, head // 2:]
            return jnp.concatenate([low * cos_t - high * sin_t, high * cos_t + low * sin_t], axis=1).astype(BF16).astype(F32)

        q0, q1, k = rope(q[:, :head]), rope(q[:, head:]), rope(k)
        groups = rows // 8

        def by_group(first, second):
            return jnp.concatenate([part8 for g in range(groups) for part8 in (first[8 * g:8 * g + 8], second[8 * g:8 * g + 8])], axis=0)

        q_all = by_group(q0, q1)
        s_new = jnp.sum(q_all * by_group(k, k), axis=1, keepdims=True)
        val_all = by_group(val, val)
        q_bf = q_all.astype(BF16)
        pos_all = by_group(pos, pos).astype(jnp.int32)
        for cp in kv_copies(c):
            cp.wait()

        def cached(i, g):
            return big[ff + 8 * ctx * g:ff + 8 * ctx * (g + 1), (2 * c + i) * head:(2 * c + i + 1) * head]

        for g in range(groups):
            sbuf[16 * g:16 * g + 16, :] = lax.dot_general(q_bf[16 * g:16 * g + 16], cached(0, g), (((1,), (1,)), ((), ())), preferred_element_type=F32)
        lane = lax.broadcasted_iota(jnp.int32, (2 * rows, 8 * ctx), 1)
        row = lax.broadcasted_iota(jnp.int32, (2 * rows, 8 * ctx), 0)
        valid = jnp.logical_and(lane // ctx == row % 8, lane % ctx < pos_all)
        s = ATTN_CAP * jnp.tanh(sbuf[:2 * rows, :] * (score_scale / ATTN_CAP))
        s_new = ATTN_CAP * jnp.tanh(s_new * (score_scale / ATTN_CAP))
        s = jnp.where(valid, s, -1e30)
        top = jnp.maximum(jnp.max(s, axis=1, keepdims=True), s_new)
        p = jnp.where(valid, jnp.exp(s - top), 0.0)
        p_new = jnp.exp(s_new - top)
        denom = jnp.sum(p, axis=1, keepdims=True) + p_new
        p_bf = p.astype(BF16)
        for g in range(groups):
            sbuf[16 * g:16 * g + 16, :head] = jnp.dot(p_bf[16 * g:16 * g + 16], cached(1, g), preferred_element_type=F32)
        o_all = (sbuf[:2 * rows, :head] + p_new.astype(BF16).astype(F32) * val_all) / denom
        o0 = jnp.concatenate([o_all[16 * g:16 * g + 8] for g in range(groups)], axis=0)
        o1 = jnp.concatenate([o_all[16 * g + 8:16 * g + 16] for g in range(groups)], axis=0)
        if c == 0:
            w_copies[3].wait()
        o = jnp.concatenate([o0, o1], axis=1).astype(BF16)
        part[c, :rows, :] = jnp.dot(o, wo[...], preferred_element_type=F32)
        if c + 1 == chunks:
            for cp in w_copies[5:]:
                cp.start()

    order = ((2, 1), (1, 2))

    def cols(h):
        return pl.ds(h * half, half)

    def rows_of(c, o):
        return pl.ds(pl.multiple_of(o * PIECES[c], 8), PIECES[c])

    def y_rows(c, o):
        return pl.ds(pl.multiple_of(group_rows(c) + o * PIECES[c], 8), PIECES[c])

    def remote(src, dst, c, phase, h, i, mask):
        return pltpu.make_async_remote_copy(src_ref=src, dst_ref=dst, send_sem=send_sem.at[c, phase, h, i], recv_sem=recv_sem.at[c, phase, h, i],
                                            device_id=(flip_t(t, mask), v), device_id_type=MESH)

    def scatter1(c, phase, h, i):
        m1, m2 = order[h]
        owner = flip_t(t, 3) if i else flip_t(t, m1)
        return remote(part.at[c, rows_of(c, owner), cols(h)], red1.at[c, h, i, pl.ds(0, PIECES[c])], c, phase, h, i, m1)

    def scatter2(c, phase, h):
        return remote(red1.at[c, h, 1, pl.ds(0, PIECES[c])], red2.at[c, h, pl.ds(0, PIECES[c])], c, phase, h, 2, order[h][1])

    def scatter_start(c, phase):
        for i in (1, 0):
            for h in range(2):
                scatter1(c, phase, h, i).start()

    def scatter_pass(c, phase):
        n = PIECES[c]
        for h in range(2):
            scatter1(c, phase, h, 1).wait_recv()
            red1[c, h, 1, :n] = red1[c, h, 1, :n] + part[c, rows_of(c, flip_t(t, order[h][1])), h * half:(h + 1) * half]
            scatter2(c, phase, h).start()

    def scatter_end(c, phase):
        n = PIECES[c]
        got = []
        for h in range(2):
            scatter1(c, phase, h, 0).wait_recv()
            scatter2(c, phase, h).wait_recv()
            got.append(part[c, rows_of(c, t), h * half:(h + 1) * half] + red1[c, h, 0, :n] + red2[c, h, :n])
        for h in range(2):
            scatter1(c, phase, h, 0).wait_send()
            scatter1(c, phase, h, 1).wait_send()
            scatter2(c, phase, h).wait_send()
        return jnp.concatenate(got, axis=1)

    def gather(c, h, i):
        m1, m2 = order[h]
        where = ybuf.at[y_rows(c, flip_t(t, m2) if i == 2 else t), cols(h)]
        return remote(where, where, c, 1, h, i, m1 if i else m2)

    def gather_start(c):
        for i in (0, 1):
            for h in range(2):
                gather(c, h, i).start()

    def gather_pass(c):
        for h in range(2):
            gather(c, h, 0).wait_recv()
            gather(c, h, 2).start()

    def gather_end(c):
        for h in range(2):
            gather(c, h, 1).wait_recv()
            gather(c, h, 2).wait_recv()
        for h in range(2):
            for i in range(3):
                gather(c, h, i).wait_send()

    def middle(c):
        attn_out = scatter_end(c, 0)
        x_own = xbuf[c, rows_of(c, t), :].astype(F32)
        x1 = (x_own + rms(attn_out, gain(g_attn_post))).astype(BF16).astype(F32)
        mid[c, :PIECES[c]] = x1
        ybuf[y_rows(c, t), :] = rms(x1, gain(g_mlp_pre)).astype(BF16).astype(F32)
        gather_start(c)

    def mlp(c):
        rows = groups_of[c]
        gather_end(c)
        if c == 0:
            for cp in w_copies[4:]:
                cp.wait()
        m = ybuf[pl.ds(group_rows(c), rows), :].astype(BF16)
        tiles = 3
        wide = ff // tiles

        def up_tile(i, carry):
            at = pl.ds(pl.multiple_of(i * wide, 128), wide)
            gate = jnp.dot(m, big[:width, at], preferred_element_type=F32)
            up = jnp.dot(m, big[width:2 * width, at], preferred_element_type=F32)
            act[:rows, at] = (jax.nn.gelu(gate, approximate=True) * up).astype(BF16)
            return carry

        lax.fori_loop(0, tiles, up_tile, 0)

        def down_tile(i, carry):
            at = pl.ds(pl.multiple_of(i * wide, 128), wide)
            part[c, :rows, at] = jnp.dot(act[:rows, :], big[2 * width:2 * width + ff, at], preferred_element_type=F32)
            return carry

        lax.fori_loop(0, tiles, down_tile, 0)
        scatter_start(c, 2)

    def finish(c):
        y = (mid[c, :PIECES[c]] + rms(scatter_end(c, 2), gain(g_mlp_post))).astype(BF16).astype(F32)
        ybuf[y_rows(c, t), :] = y
        spread(c, 0)

    def axes_of(p, bits):
        axes = [AXES[(p + s) % 3] for s in range(3)]
        mt = mv = 0
        for s in range(3):
            if bits >> s & 1:
                mt ^= FLIP[axes[s]][0]
                mv ^= FLIP[axes[s]][1]
        return mt, mv

    def block_copy(c, p, s, bits):
        mt, mv = axes_of(p, bits)
        blk = 4 * flip_v(v, mv) + flip_t(t, mt)
        at = ybuf.at[pl.ds(pl.multiple_of(bases[c] + blk * PIECES[c], 8), PIECES[c]), pl.ds(p * third, third)]
        ft, fv = FLIP['c'] if s == 3 else FLIP[AXES[(p + s) % 3]]
        i = 2 ** s - 1 + bits
        return pltpu.make_async_remote_copy(src_ref=at, dst_ref=at, send_sem=spread_send.at[c, p, i], recv_sem=spread_recv.at[c, p, i],
                                            device_id=(flip_t(t, ft), flip_v(v, fv)), device_id_type=MESH)

    def spread(c, step):
        if step == 0:
            for s in (0, 1, 2, 3):
                for p in range(3):
                    block_copy(c, p, s, 0).start()
        elif step <= 3:
            s = step - 1
            for bits in range(2 ** s):
                for p in range(3):
                    block_copy(c, p, s, bits).wait_recv()
                    for later in range(s + 1, 4):
                        block_copy(c, p, later, bits | 1 << s).start()
        else:
            for p in range(3):
                for bits in range(8):
                    block_copy(c, p, 3, bits).wait_recv()

    def spread_sent(c):
        for p in range(3):
            for s in range(4):
                for bits in range(2 ** s):
                    block_copy(c, p, s, bits).wait_send()

    sub = E_ROWS // 2
    vocab_local = e_hbm.shape[0]
    tiles = vocab_local // E_ROWS
    total = tiles * chunks

    def e_copy(i):
        return pltpu.make_async_copy(e_hbm.at[pl.ds(pl.multiple_of(i % tiles * E_ROWS, E_ROWS), E_ROWS)],
                                     big.at[pl.ds(pl.multiple_of(i % E_SLOTS * E_ROWS, E_ROWS), E_ROWS)], e_sem.at[i % E_SLOTS])

    def y_copy(c):
        return pltpu.make_async_copy(wo.at[pl.ds(0, toks_of[c])], y_hbm.at[pl.ds(bases[c], toks_of[c])], y_sem.at[c])

    def stat_copy(c, j):
        other = (me + j) % 16
        return pltpu.make_async_remote_copy(src_ref=stat.at[c], dst_ref=stats.at[c, me], send_sem=stat_send.at[c, j - 1], recv_sem=stat_recv.at[c, j - 1],
                                            device_id=(other % 4, other // 4), device_id_type=MESH)

    def reduce_rows(lg, toks, tgt, first_row):
        rel = tgt - first_row
        sublane = lax.broadcasted_iota(jnp.int32, (8, toks), 0)
        s_acc = [jnp.zeros((8, toks), F32) for _ in range(2)]
        t_acc = [jnp.zeros((8, toks), F32) for _ in range(2)]
        for r in range(sub // 8):
            th = jnp.tanh(lg[8 * r:8 * r + 8, :toks] * (1.0 / FINAL_CAP))
            s_acc[r % 2] = s_acc[r % 2] + jnp.exp(th * FINAL_CAP)
            t_acc[r % 2] = t_acc[r % 2] + jnp.where(sublane == rel - 8 * r, th, 0.0)
        return s_acc[0] + s_acc[1], t_acc[0] + t_acc[1]

    def head_pass(c, tasks):
        toks = toks_of[c]
        strip = 128
        if c:
            y_copy(c - 1).wait()
        for r in range(toks // strip):
            yv = ybuf[bases[c] + r * strip:bases[c] + (r + 1) * strip, :]
            wo[r * strip:(r + 1) * strip, :] = yv.astype(BF16)
            wq[:, r * strip:(r + 1) * strip] = rms(yv, gain(g_final)).T.astype(BF16)
        y_copy(c).start()
        first = bases[c] // 128
        tgt = jnp.concatenate([tgt_ref[first + q:first + q + 1, :] for q in range(toks // 128)], axis=1)
        tgt = jnp.broadcast_to(tgt, (8, toks)) - me * vocab_local

        def step(i, carry):
            s_sum, t_sum = carry
            n = c * tiles + i
            slot = n % E_SLOTS * E_ROWS
            e_copy(n).wait()
            lg0[:, :toks] = jnp.dot(big[pl.ds(pl.multiple_of(slot, E_ROWS // 2), sub), :], wq[:, :toks], preferred_element_type=F32)
            s_part, t_part = reduce_rows(lg1, toks, tgt, i * E_ROWS - sub)
            keep = i > 0
            s_sum = s_sum + jnp.where(keep, s_part, 0.0)
            t_sum = t_sum + jnp.where(keep, t_part, 0.0)
            lg1[:, :toks] = jnp.dot(big[pl.ds(pl.multiple_of(slot + sub, E_ROWS // 2), sub), :], wq[:, :toks], preferred_element_type=F32)
            s_part, t_part = reduce_rows(lg0, toks, tgt, i * E_ROWS)

            @pl.when(n + E_SLOTS < total)
            def _():
                e_copy(n + E_SLOTS).start()

            for at, task in tasks:
                @pl.when(i == at)
                def _(task=task):
                    task()

            return s_sum + s_part, t_sum + t_part

        zero = jnp.zeros((8, toks), F32)
        s_sum, t_sum = lax.fori_loop(0, tiles, step, (zero, zero))
        s_part, t_part = reduce_rows(lg1, toks, tgt, tiles * E_ROWS - sub)
        s_sum = jnp.sum(s_sum + s_part, axis=0, keepdims=True)
        t_sum = jnp.sum(t_sum + t_part, axis=0, keepdims=True)
        sublane = lax.broadcasted_iota(jnp.int32, (8, toks), 0)
        both = jnp.where(sublane == 0, s_sum, jnp.where(sublane == 1, t_sum, 0.0))
        stat[c, :, :toks] = both
        stats[c, me, :, :toks] = both
        for j in range(1, 16):
            stat_copy(c, j).start()

    def combine(c):
        for j in range(1, 16):
            stat_copy(c, j).wait_recv()
        tot = stats[c, 0]
        for b in range(1, 16):
            tot = tot + stats[c, b]
        lp = FINAL_CAP * tot[1:2, :] - jnp.log(tot[0:1, :])
        for q in range(toks_of[c] // 128):
            logp_ref[bases[c] // 128 + q:bases[c] // 128 + q + 1, :] = lp[:, 128 * q:128 * (q + 1)]

    attend(0)
    lg1[...] = jnp.zeros_like(lg1)
    pl.semaphore_wait(barrier, 15)
    scatter_start(0, 0)
    attend(1)
    scatter_pass(0, 0)
    scatter_start(1, 0)
    middle(0)
    scatter_pass(1, 0)
    gather_pass(0)
    middle(1)
    mlp(0)
    gather_pass(1)
    scatter_pass(0, 2)
    mlp(1)
    for i in range(E_SLOTS):
        e_copy(i).start()
    finish(0)
    scatter_pass(1, 2)
    spread(0, 1)
    spread(0, 2)
    spread(0, 3)
    spread(0, 4)
    head_pass(0, ((0, lambda: finish(1)), (3, lambda: spread(1, 1)), (6, lambda: spread(1, 2)), (10, lambda: spread(1, 3)), (13, lambda: spread(1, 4))))
    head_pass(1, ((2, lambda: combine(0)),))
    combine(1)
    for c in range(chunks):
        spread_sent(c)
        for j in range(1, 16):
            stat_copy(c, j).wait_send()
    y_copy(chunks - 1).wait()


def step_kernel(x, seq, tgt, freq, gains, w_q, w_k, w_v, w_o, w_gate, w_up, w_down, k_rows, v_rows, table):
    tokens, width = x.shape
    chunks = len(PIECES)
    top = max(PIECES)
    rows, toks = 4 * top, 16 * top
    head = w_k.shape[1]
    ctx = k_rows.shape[0] // tokens
    ff = w_gate.shape[1]
    vm = pl.BlockSpec(memory_space=pltpu.VMEM)
    hbm = pl.BlockSpec(memory_space=pl.ANY)
    dma = pltpu.SemaphoreType.DMA
    return pl.pallas_call(
        kernel,
        out_shape=(jax.ShapeDtypeStruct((tokens // 128, 128), F32), jax.ShapeDtypeStruct((tokens, width), BF16)),
        in_specs=[hbm] + [vm] * 8 + [hbm] * 10,
        out_specs=(vm, hbm),
        scratch_shapes=[
            pltpu.VMEM((chunks, rows, width), BF16),
            pltpu.VMEM(w_q.shape, BF16),
            pltpu.VMEM(w_k.shape, BF16),
            pltpu.VMEM(w_v.shape, BF16),
            pltpu.VMEM(w_o.shape, BF16),
            pltpu.VMEM((2 * width + ff, ff), BF16),
            pltpu.VMEM((2 * rows, 8 * ctx), F32),
            pltpu.VMEM((chunks, rows, width), F32),
            pltpu.VMEM((chunks, 2, 2, top, width // 2), F32),
            pltpu.VMEM((chunks, 2, top, width // 2), F32),
            pltpu.VMEM((tokens, width), F32),
            pltpu.VMEM((chunks, top, width), F32),
            pltpu.VMEM((rows, ff), BF16),
            pltpu.VMEM((E_ROWS // 2, toks), F32),
            pltpu.VMEM((E_ROWS // 2, toks), F32),
            pltpu.VMEM((chunks, 8, toks), F32),
            pltpu.VMEM((chunks, 16, 8, toks), F32),
            dma((chunks,)),
            dma((7,)),
            dma((chunks, 2)),
            dma((E_SLOTS,)),
            dma((chunks,)),
            dma((chunks, 3, 2, 3)),
            dma((chunks, 3, 2, 3)),
            dma((chunks, 3, 15)),
            dma((chunks, 3, 15)),
            dma((chunks, 15)),
            dma((chunks, 15)),
        ],
        compiler_params=pltpu.CompilerParams(collective_id=0, has_side_effects=True, vmem_limit_bytes=67_000_000),
        name='step',
    )(x, seq, tgt, freq, *gains, w_q, w_k, w_v, w_o, w_gate, w_up, w_down, k_rows, v_rows, table)


def solution(mesh):
    in_specs = (P(), P(), P(), P(), P(None, 't'), P(None, 't'), P(None, 't'), P('t', None), P(), P(), P(None, 't'), P(None, 't'), P('t', None), P(), P(), P(None, None, 't', None), P(None, None, 't', None), P(('v', 't'), None))

    def local_step(hidden_in, seq_lens, target, g_attn_pre, w_q, w_k, w_v, w_o, g_attn_post, g_mlp_pre, w_gate, w_up, w_down, g_mlp_post, g_final, k_cache, v_cache, embed_table):
        tokens = hidden_in.shape[0]
        ctx, _, head_dim = k_cache.shape[1:]
        freq = ROPE_BASE ** (-2.0 * np.arange(head_dim // 2, dtype=np.float32) / head_dim)
        logp, hidden_out = step_kernel(
            hidden_in, seq_lens.reshape(-1, 128), target.reshape(-1, 128), jnp.asarray(freq[None, :], F32),
            (g_attn_pre, g_attn_post, g_mlp_pre, g_mlp_post, g_final), w_q, w_k, w_v, w_o, w_gate, w_up, w_down,
            k_cache.reshape(tokens * ctx, head_dim), v_cache.reshape(tokens * ctx, head_dim), embed_table)
        return logp.reshape(tokens), hidden_out

    return jax.shard_map(local_step, mesh=mesh, in_specs=in_specs, out_specs=(P(), P()), check_vma=False)
```

time: 218 us -> 201 us (0.922)
  Pallas kernels: 202 us -> 194 us
  local copies, waits for them, and re-layouts: 12.3 us -> 6.1 us
  other arithmetic: 2.57 us -> 0 us
    pallas_call x2 -> x1, Pallas kernels: 202 us -> 194 us  [step_kernel(): pl.pallas_call(kernel, out_shape=(jax.ShapeDtypeStruct((tokens // 128, 12...]
    another operation x6 -> x0, local copies, waits for them, and re-layouts: 3.57 us -> none  [local_step(): jnp.stack([g_attn_pre, g_attn_post, g_mlp_pre, g_mlp_post, g_final])]
    reshape x6 -> x0, local copies, waits for them, and re-layouts: 2.29 us -> none  [the longest x2 1.44 us: local_step(): target.reshape(16, CHUNKS, piece).transpose(1, 0, 2)]
    unnamed x1 -> x2, local copies, waits for them, and re-layouts: 4.82 us -> 6.1 us
where the time goes in v2:
time: 201 us
  Pallas kernels  194 us (97%)
  local copies, waits for them, and re-layouts  6.1 us (3%)
    pallas_call x1, Pallas kernels, step_kernel(): pl.pallas_call(kernel, out_shape=(jax.ShapeDtypeStruct((tokens // 128, 12...  194 us
    unnamed x2, local copies, waits for them, and re-layouts  6.1 us

profile of v2, /device:TPU:0, one launch (start us, length us, event | category | flops | bytes accessed | tf_op | source)
XLA Modules:
  0.0 200.8 jit_solution(9802081918122179264)
XLA Ops:
  0.6 194.0 %step.1 = (f32[8,128]{1,0:T(8,128)}, bf16[1024,2304]{1,0:T(8,128)(2,1)}) custom-call(bf16[1024,2304]{1,0:T(8,128)(2,1)} %x_hbm.1, s32[8,128]{1,0:T(8,128)} %bitcast.7, s32[8,128]{1,0:T(8,128)} %bitcast.8, f32[1,128]{1,0:T(1,128)} %constant.2.clone.freq_ref, bf16[2304]{0:T(1024)(128)(2,1)} %g_attn_pre.1, bf16[2304]{0:T(1024)(128)(2,1)} %g_attn_post.1, ...), custom_call_target="tpu_custom_call" | custom-call | tf_op jit(solution)/shard_map/step/pallas_call | solution.py:443
  194.7 1.3 copy.23
  196.0 4.8 %copy.24 = bf16[1024,2304]{1,0:T(8,128)(2,1)} copy(bf16[1024,2304]{1,0:T(8,128)(2,1)} %get-tuple-element.9) | data formatting | bytes 9437184

commit v3 on v2

--- a/solution.py
+++ b/solution.py
@@ -15,8 +15,8 @@
 BF16 = jnp.bfloat16
 
 PIECES = (32, 32)
-E_ROWS = 800
-E_SLOTS = 8
+E_ROWS = 1600
+E_SLOTS = 4
 AXES = ('x', 'z', 'y')
 FLIP = {'x': (0, 2), 'y': (1, 0), 'z': (2, 0), 'c': (0, 1)}
 
@@ -233,7 +233,6 @@
         x1 = (x_own + rms(attn_out, gain(g_attn_post))).astype(BF16).astype(F32)
         mid[c, :PIECES[c]] = x1
         ybuf[y_rows(c, t), :] = rms(x1, gain(g_mlp_pre)).astype(BF16).astype(F32)
-        gather_start(c)
 
     def mlp(c):
         rows = groups_of[c]
@@ -260,7 +259,6 @@
             return carry
 
         lax.fori_loop(0, tiles, down_tile, 0)
-        scatter_start(c, 2)
 
     def finish(c):
         y = (mid[c, :PIECES[c]] + rms(scatter_end(c, 2), gain(g_mlp_post))).astype(BF16).astype(F32)
@@ -308,7 +306,7 @@
                 for bits in range(2 ** s):
                     block_copy(c, p, s, bits).wait_send()
 
-    sub = E_ROWS // 2
+    sub = E_ROWS // 4
     vocab_local = e_hbm.shape[0]
     tiles = vocab_local // E_ROWS
     total = tiles * chunks
@@ -355,13 +353,13 @@
             n = c * tiles + i
             slot = n % E_SLOTS * E_ROWS
             e_copy(n).wait()
-            lg0[:, :toks] = jnp.dot(big[pl.ds(pl.multiple_of(slot, E_ROWS // 2), sub), :], wq[:, :toks], preferred_element_type=F32)
-            s_part, t_part = reduce_rows(lg1, toks, tgt, i * E_ROWS - sub)
-            keep = i > 0
-            s_sum = s_sum + jnp.where(keep, s_part, 0.0)
-            t_sum = t_sum + jnp.where(keep, t_part, 0.0)
-            lg1[:, :toks] = jnp.dot(big[pl.ds(pl.multiple_of(slot + sub, E_ROWS // 2), sub), :], wq[:, :toks], preferred_element_type=F32)
-            s_part, t_part = reduce_rows(lg0, toks, tgt, i * E_ROWS)
+            for j in range(4):
+                now, before = (lg0, lg1) if j % 2 == 0 else (lg1, lg0)
+                now[:, :toks] = jnp.dot(big[pl.ds(pl.multiple_of(slot + j * sub, sub), sub), :], wq[:, :toks], preferred_element_type=F32)
+                s_part, t_part = reduce_rows(before, toks, tgt, i * E_ROWS + (j - 1) * sub)
+                if j == 0:
+                    s_part, t_part = jnp.where(i > 0, s_part, 0.0), jnp.where(i > 0, t_part, 0.0)
+                s_sum, t_sum = s_sum + s_part, t_sum + t_part
 
             @pl.when(n + E_SLOTS < total)
             def _():
@@ -372,7 +370,7 @@
                 def _(task=task):
                     task()
 
-            return s_sum + s_part, t_sum + t_part
+            return s_sum, t_sum
 
         zero = jnp.zeros((8, toks), F32)
         s_sum, t_sum = lax.fori_loop(0, tiles, step, (zero, zero))
@@ -404,22 +402,25 @@
     scatter_pass(0, 0)
     scatter_start(1, 0)
     middle(0)
+    gather_start(0)
     scatter_pass(1, 0)
     gather_pass(0)
     middle(1)
+    gather_start(1)
     mlp(0)
+    scatter_start(0, 2)
+    scatter_pass(0, 2)
     gather_pass(1)
-    scatter_pass(0, 2)
+    finish(0)
+    spread(0, 1)
     mlp(1)
     for i in range(E_SLOTS):
         e_copy(i).start()
-    finish(0)
-    scatter_pass(1, 2)
-    spread(0, 1)
     spread(0, 2)
     spread(0, 3)
     spread(0, 4)
-    head_pass(0, ((0, lambda: finish(1)), (3, lambda: spread(1, 1)), (6, lambda: spread(1, 2)), (10, lambda: spread(1, 3)), (13, lambda: spread(1, 4))))
+    scatter_start(1, 2)
+    head_pass(0, ((0, lambda: scatter_pass(1, 2)), (2, lambda: finish(1)), (3, lambda: spread(1, 1)), (5, lambda: spread(1, 2)), (7, lambda: spread(1, 3)), (9, lambda: spread(1, 4))))
     head_pass(1, ((2, lambda: combine(0)),))
     combine(1)
     for c in range(chunks):
@@ -459,8 +460,8 @@
             pltpu.VMEM((tokens, width), F32),
             pltpu.VMEM((chunks, top, width), F32),
             pltpu.VMEM((rows, ff), BF16),
-            pltpu.VMEM((E_ROWS // 2, toks), F32),
-            pltpu.VMEM((E_ROWS // 2, toks), F32),
+            pltpu.VMEM((E_ROWS // 4, toks), F32),
+            pltpu.VMEM((E_ROWS // 4, toks), F32),
             pltpu.VMEM((chunks, 8, toks), F32),
             pltpu.VMEM((chunks, 16, 8, toks), F32),
             dma((chunks,)),

time: 201 us -> 181 us (0.900)
  Pallas kernels: 194 us -> 174 us
    pallas_call x1, Pallas kernels: 194 us -> 174 us  [step_kernel(): pl.pallas_call(kernel, out_shape=(jax.ShapeDtypeStruct((tokens // 128, 12...]
where the time goes in v3:
time: 181 us; the launch traced here: 180 us
  Pallas kernels  174 us (96%)
  local copies, waits for them, and re-layouts  6.1 us (3%)
    pallas_call x1, Pallas kernels, step_kernel(): pl.pallas_call(kernel, out_shape=(jax.ShapeDtypeStruct((tokens // 128, 12...  174 us
    unnamed x2, local copies, waits for them, and re-layouts  6.1 us

profile of v3, /device:TPU:0, one launch (start us, length us, event | category | flops | bytes accessed | tf_op | source)
XLA Modules:
  0.0 180.3 jit_solution(3369392633335984182)
XLA Ops:
  0.6 173.5 %step.1 = (f32[8,128]{1,0:T(8,128)}, bf16[1024,2304]{1,0:T(8,128)(2,1)}) custom-call(bf16[1024,2304]{1,0:T(8,128)(2,1)} %x_hbm.1, s32[8,128]{1,0:T(8,128)} %bitcast.7, s32[8,128]{1,0:T(8,128)} %bitcast.8, f32[1,128]{1,0:T(1,128)} %constant.2.clone.freq_ref, bf16[2304]{0:T(1024)(128)(2,1)} %g_attn_pre.1, bf16[2304]{0:T(1024)(128)(2,1)} %g_attn_post.1, ...), custom_call_target="tpu_custom_call" | custom-call | tf_op jit(solution)/shard_map/step/pallas_call | solution.py:444
  174.2 1.3 copy.23
  175.5 4.8 %copy.24 = bf16[1024,2304]{1,0:T(8,128)(2,1)} copy(bf16[1024,2304]{1,0:T(8,128)(2,1)} %get-tuple-element.9) | data formatting | bytes 9437184

commit v4 on v3

--- a/solution.py
+++ b/solution.py
@@ -40,8 +40,8 @@
 
 
 def kernel(x_hbm, seq_ref, tgt_ref, freq_ref, g_attn_pre, g_attn_post, g_mlp_pre, g_mlp_post, g_final,
-           wq_hbm, wk_hbm, wv_hbm, wo_hbm, wg_hbm, wu_hbm, wd_hbm, k_hbm, v_hbm, e_hbm, logp_ref, y_hbm,
-           xbuf, wq, wk, wv, wo, big, sbuf, part, red1, red2, ybuf, mid, act, lg0, lg1, stat, stats,
+           wq_hbm, wk_hbm, wv_hbm, wo_hbm, wg_hbm, wu_hbm, wd_hbm, k_hbm, v_hbm, e_hbm, stats, y_hbm,
+           xbuf, wq, wk, wv, wo, big, sbuf, part, red1, red2, ybuf, mid, act, lg0, lg1, stat,
            x_sem, w_sem, kv_sem, e_sem, y_sem, send_sem, recv_sem, spread_send, spread_recv, stat_send, stat_recv):
     t = lax.axis_index('t')
     v = lax.axis_index('v')
@@ -179,9 +179,9 @@
     def scatter2(c, phase, h):
         return remote(red1.at[c, h, 1, pl.ds(0, PIECES[c])], red2.at[c, h, pl.ds(0, PIECES[c])], c, phase, h, 2, order[h][1])
 
-    def scatter_start(c, phase):
+    def scatter_start(c, phase, halves=(0, 1)):
         for i in (1, 0):
-            for h in range(2):
+            for h in halves:
                 scatter1(c, phase, h, i).start()
 
     def scatter_pass(c, phase):
@@ -234,7 +234,7 @@
         mid[c, :PIECES[c]] = x1
         ybuf[y_rows(c, t), :] = rms(x1, gain(g_mlp_pre)).astype(BF16).astype(F32)
 
-    def mlp(c):
+    def mlp(c, send):
         rows = groups_of[c]
         gather_end(c)
         if c == 0:
@@ -253,12 +253,10 @@
 
         lax.fori_loop(0, tiles, up_tile, 0)
 
-        def down_tile(i, carry):
-            at = pl.ds(pl.multiple_of(i * wide, 128), wide)
-            part[c, :rows, at] = jnp.dot(act[:rows, :], big[2 * width:2 * width + ff, at], preferred_element_type=F32)
-            return carry
-
-        lax.fori_loop(0, tiles, down_tile, 0)
+        for h in range(2):
+            part[c, :rows, h * half:(h + 1) * half] = jnp.dot(act[:rows, :], big[2 * width:2 * width + ff, h * half:(h + 1) * half], preferred_element_type=F32)
+            if send:
+                scatter_start(c, 2, (h,))
 
     def finish(c):
         y = (mid[c, :PIECES[c]] + rms(scatter_end(c, 2), gain(g_mlp_post))).astype(BF16).astype(F32)
@@ -334,7 +332,7 @@
             t_acc[r % 2] = t_acc[r % 2] + jnp.where(sublane == rel - 8 * r, th, 0.0)
         return s_acc[0] + s_acc[1], t_acc[0] + t_acc[1]
 
-    def head_pass(c, tasks):
+    def head_pass(c, per, tasks):
         toks = toks_of[c]
         strip = 128
         if c:
@@ -342,7 +340,7 @@
         for r in range(toks // strip):
             yv = ybuf[bases[c] + r * strip:bases[c] + (r + 1) * strip, :]
             wo[r * strip:(r + 1) * strip, :] = yv.astype(BF16)
-            wq[:, r * strip:(r + 1) * strip] = rms(yv, gain(g_final)).T.astype(BF16)
+            wq[:, r * strip:(r + 1) * strip] = rms(yv, gain(g_final)).astype(BF16).T
         y_copy(c).start()
         first = bases[c] // 128
         tgt = jnp.concatenate([tgt_ref[first + q:first + q + 1, :] for q in range(toks // 128)], axis=1)
@@ -350,20 +348,22 @@
 
         def step(i, carry):
             s_sum, t_sum = carry
-            n = c * tiles + i
-            slot = n % E_SLOTS * E_ROWS
-            e_copy(n).wait()
-            for j in range(4):
+            n = c * tiles + i * per
+            for k in range(per):
+                e_copy(n + k).wait()
+            for j in range(4 * per):
                 now, before = (lg0, lg1) if j % 2 == 0 else (lg1, lg0)
-                now[:, :toks] = jnp.dot(big[pl.ds(pl.multiple_of(slot + j * sub, sub), sub), :], wq[:, :toks], preferred_element_type=F32)
-                s_part, t_part = reduce_rows(before, toks, tgt, i * E_ROWS + (j - 1) * sub)
+                at = (n + j // 4) % E_SLOTS * E_ROWS + j % 4 * sub
+                now[:, :toks] = jnp.dot(big[pl.ds(pl.multiple_of(at, sub), sub), :], wq[:, :toks], preferred_element_type=F32)
+                s_part, t_part = reduce_rows(before, toks, tgt, i * per * E_ROWS + (j - 1) * sub)
                 if j == 0:
                     s_part, t_part = jnp.where(i > 0, s_part, 0.0), jnp.where(i > 0, t_part, 0.0)
                 s_sum, t_sum = s_sum + s_part, t_sum + t_part
 
-            @pl.when(n + E_SLOTS < total)
-            def _():
-                e_copy(n + E_SLOTS).start()
+            for k in range(per):
+                @pl.when(n + k + E_SLOTS < total)
+                def _(k=k):
+                    e_copy(n + k + E_SLOTS).start()
 
             for at, task in tasks:
                 @pl.when(i == at)
@@ -373,26 +373,16 @@
             return s_sum, t_sum
 
         zero = jnp.zeros((8, toks), F32)
-        s_sum, t_sum = lax.fori_loop(0, tiles, step, (zero, zero))
+        s_sum, t_sum = lax.fori_loop(0, tiles // per, step, (zero, zero))
         s_part, t_part = reduce_rows(lg1, toks, tgt, tiles * E_ROWS - sub)
         s_sum = jnp.sum(s_sum + s_part, axis=0, keepdims=True)
         t_sum = jnp.sum(t_sum + t_part, axis=0, keepdims=True)
-        sublane = lax.broadcasted_iota(jnp.int32, (8, toks), 0)
-        both = jnp.where(sublane == 0, s_sum, jnp.where(sublane == 1, t_sum, 0.0))
-        stat[c, :, :toks] = both
-        stats[c, me, :, :toks] = both
+        rows8 = [z[:, 128 * q:128 * (q + 1)] for z in (s_sum, t_sum) for q in range(toks // 128)]
+        both = jnp.concatenate(rows8, axis=0)
+        stat[c] = both
+        stats[c, me] = both
         for j in range(1, 16):
             stat_copy(c, j).start()
-
-    def combine(c):
-        for j in range(1, 16):
-            stat_copy(c, j).wait_recv()
-        tot = stats[c, 0]
-        for b in range(1, 16):
-            tot = tot + stats[c, b]
-        lp = FINAL_CAP * tot[1:2, :] - jnp.log(tot[0:1, :])
-        for q in range(toks_of[c] // 128):
-            logp_ref[bases[c] // 128 + q:bases[c] // 128 + q + 1, :] = lp[:, 128 * q:128 * (q + 1)]
 
     attend(0)
     lg1[...] = jnp.zeros_like(lg1)
@@ -407,27 +397,72 @@
     gather_pass(0)
     middle(1)
     gather_start(1)
-    mlp(0)
-    scatter_start(0, 2)
+    mlp(0, True)
     scatter_pass(0, 2)
     gather_pass(1)
     finish(0)
     spread(0, 1)
-    mlp(1)
+    mlp(1, False)
     for i in range(E_SLOTS):
         e_copy(i).start()
     spread(0, 2)
     spread(0, 3)
     spread(0, 4)
     scatter_start(1, 2)
-    head_pass(0, ((0, lambda: scatter_pass(1, 2)), (2, lambda: finish(1)), (3, lambda: spread(1, 1)), (5, lambda: spread(1, 2)), (7, lambda: spread(1, 3)), (9, lambda: spread(1, 4))))
-    head_pass(1, ((2, lambda: combine(0)),))
-    combine(1)
+    head_pass(0, 1, ((0, lambda: scatter_pass(1, 2)), (2, lambda: finish(1)), (3, lambda: spread(1, 1)), (5, lambda: spread(1, 2)), (7, lambda: spread(1, 3)), (9, lambda: spread(1, 4))))
+    head_pass(1, 2, ())
     for c in range(chunks):
         spread_sent(c)
         for j in range(1, 16):
+            stat_copy(c, j).wait_recv()
             stat_copy(c, j).wait_send()
     y_copy(chunks - 1).wait()
+
+
+def out_kernel(stats_hbm, y_hbm, logp_hbm, out_hbm, stats, logp, ybuf, stat_sem, in_sem, out_sem):
+    pieces = in_sem.shape[0]
+    n = ybuf.shape[0] // pieces
+    get = pltpu.make_async_copy(stats_hbm, stats, stat_sem.at[0])
+    get.start()
+
+    def y_in(i):
+        return pltpu.make_async_copy(y_hbm.at[pl.ds(i * n, n)], ybuf.at[pl.ds(i * n, n)], in_sem.at[i])
+
+    def y_out(i):
+        return pltpu.make_async_copy(ybuf.at[pl.ds(i * n, n)], out_hbm.at[pl.ds(i * n, n)], out_sem.at[i])
+
+    for i in range(pieces):
+        y_in(i).start()
+    get.wait()
+    first = 0
+    for c, piece in enumerate(PIECES):
+        tot = stats[c, 0]
+        for b in range(1, stats.shape[1]):
+            tot = tot + stats[c, b]
+        rows = piece * 16 // 128
+        logp[first:first + rows, :] = FINAL_CAP * tot[rows:2 * rows] - jnp.log(tot[:rows])
+        first += rows
+    put = pltpu.make_async_copy(logp, logp_hbm, stat_sem.at[1])
+    put.start()
+    for i in range(pieces):
+        y_in(i).wait()
+        y_out(i).start()
+    put.wait()
+    for i in range(pieces):
+        y_out(i).wait()
+
+
+def collect(stats, y):
+    hbm = pl.BlockSpec(memory_space=pl.ANY)
+    dma = pltpu.SemaphoreType.DMA
+    return pl.pallas_call(
+        out_kernel,
+        out_shape=(jax.ShapeDtypeStruct((y.shape[0] // 128, 128), F32), jax.ShapeDtypeStruct(y.shape, y.dtype)),
+        in_specs=[hbm, hbm],
+        out_specs=(hbm, hbm),
+        scratch_shapes=[pltpu.VMEM(stats.shape, F32), pltpu.VMEM((y.shape[0] // 128, 128), F32), pltpu.VMEM(y.shape, y.dtype), dma((2,)), dma((8,)), dma((8,))],
+        name='collect',
+    )(stats, y)
 
 
 def step_kernel(x, seq, tgt, freq, gains, w_q, w_k, w_v, w_o, w_gate, w_up, w_down, k_rows, v_rows, table):
@@ -443,7 +478,7 @@
     dma = pltpu.SemaphoreType.DMA
     return pl.pallas_call(
         kernel,
-        out_shape=(jax.ShapeDtypeStruct((tokens // 128, 128), F32), jax.ShapeDtypeStruct((tokens, width), BF16)),
+        out_shape=(jax.ShapeDtypeStruct((chunks, 16, 8, 128), F32), jax.ShapeDtypeStruct((tokens, width), BF16)),
         in_specs=[hbm] + [vm] * 8 + [hbm] * 10,
         out_specs=(vm, hbm),
         scratch_shapes=[
@@ -462,8 +497,7 @@
             pltpu.VMEM((rows, ff), BF16),
             pltpu.VMEM((E_ROWS // 4, toks), F32),
             pltpu.VMEM((E_ROWS // 4, toks), F32),
-            pltpu.VMEM((chunks, 8, toks), F32),
-            pltpu.VMEM((chunks, 16, 8, toks), F32),
+            pltpu.VMEM((chunks, 8, 128), F32),
             dma((chunks,)),
             dma((7,)),
             dma((chunks, 2)),
@@ -488,10 +522,11 @@
         tokens = hidden_in.shape[0]
         ctx, _, head_dim = k_cache.shape[1:]
         freq = ROPE_BASE ** (-2.0 * np.arange(head_dim // 2, dtype=np.float32) / head_dim)
-        logp, hidden_out = step_kernel(
+        stats, y = step_kernel(
             hidden_in, seq_lens.reshape(-1, 128), target.reshape(-1, 128), jnp.asarray(freq[None, :], F32),
             (g_attn_pre, g_attn_post, g_mlp_pre, g_mlp_post, g_final), w_q, w_k, w_v, w_o, w_gate, w_up, w_down,
             k_cache.reshape(tokens * ctx, head_dim), v_cache.reshape(tokens * ctx, head_dim), embed_table)
+        logp, hidden_out = collect(stats, y)
         return logp.reshape(tokens), hidden_out
 
     return jax.shard_map(local_step, mesh=mesh, in_specs=in_specs, out_specs=(P(), P()), check_vma=False)

time: 181 us -> 177 us (0.978)
  local copies, waits for them, and re-layouts: 6.1 us -> 0 us
  Pallas kernels: 174 us -> 176 us
    unnamed x2 -> x0, local copies, waits for them, and re-layouts: 6.1 us -> none
    pallas_call x1 -> x2, Pallas kernels: 174 us -> 176 us  [the longest x1 171 us: step_kernel(): pl.pallas_call(kernel, out_shape=(jax.ShapeDtypeStruct((chunks, 16, 8, 12...]
where the time goes in v4:
time: 177 us; the launch traced here: 176 us
  Pallas kernels  176 us (99%)
    pallas_call x1, Pallas kernels, step_kernel(): pl.pallas_call(kernel, out_shape=(jax.ShapeDtypeStruct((chunks, 16, 8, 12...  171 us
    pallas_call x1, Pallas kernels, collect(): pl.pallas_call(out_kernel, out_shape=(jax.ShapeDtypeStruct((y.shape[0] //...  4.51 us

profile of v4, /device:TPU:0, one launch (start us, length us, event | category | flops | bytes accessed | tf_op | source)
XLA Modules:
  0.0 176.4 jit_solution(5611903190059913228)
XLA Ops:
  0.6 171.0 %step.1 = (f32[2,16,8,128]{3,2,1,0:T(8,128)}, bf16[1024,2304]{1,0:T(8,128)(2,1)}) custom-call(bf16[1024,2304]{1,0:T(8,128)(2,1)} %x_hbm.1, s32[8,128]{1,0:T(8,128)} %bitcast.7, s32[8,128]{1,0:T(8,128)} %bitcast.8, f32[1,128]{1,0:T(1,128)} %constant.2.clone.freq_ref, bf16[2304]{0:T(1024)(128)(2,1)} %g_attn_pre.1, bf16[2304]{0:T(1024)(128)(2,1)} %g_attn_post.1, ...), custom_call_target="tpu_custom_call" | custom-call | tf_op jit(solution)/shard_map/step/pallas_call | solution.py:479
  171.7 4.5 %collect.1 = (f32[8,128]{1,0:T(8,128)}, bf16[1024,2304]{1,0:T(8,128)(2,1)}) custom-call(f32[2,16,8,128]{3,2,1,0:T(8,128)} %get-tuple-element.6.stats_hbm, bf16[1024,2304]{1,0:T(8,128)(2,1)} %get-tuple-element.7.y_hbm), custom_call_target="tpu_custom_call" | custom-call | tf_op jit(solution)/shard_map/collect/pallas_call | solution.py:458

commit v5 on v4

--- a/solution.py
+++ b/solution.py
@@ -321,6 +321,9 @@
         return pltpu.make_async_remote_copy(src_ref=stat.at[c], dst_ref=stats.at[c, me], send_sem=stat_send.at[c, j - 1], recv_sem=stat_recv.at[c, j - 1],
                                             device_id=(other % 4, other // 4), device_id_type=MESH)
 
+    def own_stat(c):
+        return pltpu.make_async_copy(stat.at[c], stats.at[c, me], y_sem.at[chunks + c])
+
     def reduce_rows(lg, toks, tgt, first_row):
         rel = tgt - first_row
         sublane = lax.broadcasted_iota(jnp.int32, (8, toks), 0)
@@ -380,7 +383,7 @@
         rows8 = [z[:, 128 * q:128 * (q + 1)] for z in (s_sum, t_sum) for q in range(toks // 128)]
         both = jnp.concatenate(rows8, axis=0)
         stat[c] = both
-        stats[c, me] = both
+        own_stat(c).start()
         for j in range(1, 16):
             stat_copy(c, j).start()
 
@@ -406,13 +409,14 @@
     for i in range(E_SLOTS):
         e_copy(i).start()
     spread(0, 2)
+    scatter_start(1, 2)
     spread(0, 3)
     spread(0, 4)
-    scatter_start(1, 2)
-    head_pass(0, 1, ((0, lambda: scatter_pass(1, 2)), (2, lambda: finish(1)), (3, lambda: spread(1, 1)), (5, lambda: spread(1, 2)), (7, lambda: spread(1, 3)), (9, lambda: spread(1, 4))))
+    head_pass(0, 1, ((0, lambda: scatter_pass(1, 2)), (2, lambda: finish(1)), (4, lambda: spread(1, 1)), (6, lambda: spread(1, 2)), (8, lambda: spread(1, 3)), (9, lambda: spread(1, 4))))
     head_pass(1, 2, ())
     for c in range(chunks):
         spread_sent(c)
+        own_stat(c).wait()
         for j in range(1, 16):
             stat_copy(c, j).wait_recv()
             stat_copy(c, j).wait_send()
@@ -480,7 +484,7 @@
         kernel,
         out_shape=(jax.ShapeDtypeStruct((chunks, 16, 8, 128), F32), jax.ShapeDtypeStruct((tokens, width), BF16)),
         in_specs=[hbm] + [vm] * 8 + [hbm] * 10,
-        out_specs=(vm, hbm),
+        out_specs=(hbm, hbm),
         scratch_shapes=[
             pltpu.VMEM((chunks, rows, width), BF16),
             pltpu.VMEM(w_q.shape, BF16),
@@ -502,7 +506,7 @@
             dma((7,)),
             dma((chunks, 2)),
             dma((E_SLOTS,)),
-            dma((chunks,)),
+            dma((2 * chunks,)),
             dma((chunks, 3, 2, 3)),
             dma((chunks, 3, 2, 3)),
             dma((chunks, 3, 15)),

time: 177 us -> 177 us (level)
  no operation moved by 1% of the time
where the time goes in v5:
time: 177 us
  Pallas kernels  176 us (99%)
    pallas_call x1, Pallas kernels, step_kernel(): pl.pallas_call(kernel, out_shape=(jax.ShapeDtypeStruct((chunks, 16, 8, 12...  172 us
    pallas_call x1, Pallas kernels, collect(): pl.pallas_call(out_kernel, out_shape=(jax.ShapeDtypeStruct((y.shape[0] //...  4.51 us

profile of v5, /device:TPU:0, one launch (start us, length us, event | category | flops | bytes accessed | tf_op | source)
XLA Modules:
  0.0 177.0 jit_solution(6623331277726284631)
XLA Ops:
  0.6 171.6 %step.1 = (f32[2,16,8,128]{3,2,1,0:T(8,128)}, bf16[1024,2304]{1,0:T(8,128)(2,1)}) custom-call(bf16[1024,2304]{1,0:T(8,128)(2,1)} %x_hbm.1, s32[8,128]{1,0:T(8,128)} %bitcast.7, s32[8,128]{1,0:T(8,128)} %bitcast.8, f32[1,128]{1,0:T(1,128)} %constant.2.clone.freq_ref, bf16[2304]{0:T(1024)(128)(2,1)} %g_attn_pre.1, bf16[2304]{0:T(1024)(128)(2,1)} %g_attn_post.1, ...), custom_call_target="tpu_custom_call" | custom-call | tf_op jit(solution)/shard_map/step/pallas_call | solution.py:483
  172.3 4.5 %collect.1 = (f32[8,128]{1,0:T(8,128)}, bf16[1024,2304]{1,0:T(8,128)(2,1)}) custom-call(f32[2,16,8,128]{3,2,1,0:T(8,128)} %get-tuple-element.6.stats_hbm, bf16[1024,2304]{1,0:T(8,128)(2,1)} %get-tuple-element.7.y_hbm), custom_call_target="tpu_custom_call" | custom-call | tf_op jit(solution)/shard_map/collect/pallas_call | solution.py:462

commit v6 on v4

--- a/solution.py
+++ b/solution.py
@@ -77,14 +77,6 @@
     x_copies[0].start()
     for cp in w_copies[:3]:
         cp.start()
-    for cp in kv_copies(0):
-        cp.start()
-    w_copies[3].start()
-    for c in range(1, chunks):
-        x_copies[c].start()
-        for cp in kv_copies(c):
-            cp.start()
-    w_copies[4].start()
 
     barrier = pltpu.get_barrier_semaphore()
     for j in range(1, 16):
@@ -94,10 +86,18 @@
     def attend(c):
         rows = groups_of[c]
         x_copies[c].wait()
+        if c == 0:
+            for cp in kv_copies(0):
+                cp.start()
         a = rms(xbuf[c, :rows, :].astype(F32), gain(g_attn_pre)).astype(BF16)
         if c == 0:
             for cp in w_copies[:3]:
                 cp.wait()
+            w_copies[3].start()
+            for later in range(1, chunks):
+                x_copies[later].start()
+                for cp in kv_copies(later):
+                    cp.start()
         q = jnp.dot(a, wq[...], preferred_element_type=F32)
         k = jnp.dot(a, wk[...], preferred_element_type=F32)
         val = jnp.dot(a, wv[...], preferred_element_type=F32).astype(BF16).astype(F32)
@@ -153,7 +153,7 @@
         o = jnp.concatenate([o0, o1], axis=1).astype(BF16)
         part[c, :rows, :] = jnp.dot(o, wo[...], preferred_element_type=F32)
         if c + 1 == chunks:
-            for cp in w_copies[5:]:
+            for cp in w_copies[4:]:
                 cp.start()
 
     order = ((2, 1), (1, 2))

time: 177 us -> 177 us (level)
  no operation moved by 1% of the time
where the time goes in v6:
time: 177 us
  Pallas kernels  176 us (99%)
    pallas_call x1, Pallas kernels, step_kernel(): pl.pallas_call(kernel, out_shape=(jax.ShapeDtypeStruct((chunks, 16, 8, 12...  171 us
    pallas_call x1, Pallas kernels, collect(): pl.pallas_call(out_kernel, out_shape=(jax.ShapeDtypeStruct((y.shape[0] //...  4.51 us

profile of v6, /device:TPU:0, one launch (start us, length us, event | category | flops | bytes accessed | tf_op | source)
XLA Modules:
  0.0 176.5 jit_solution(18404692271047690678)
XLA Ops:
  0.6 171.2 %step.1 = (f32[2,16,8,128]{3,2,1,0:T(8,128)}, bf16[1024,2304]{1,0:T(8,128)(2,1)}) custom-call(bf16[1024,2304]{1,0:T(8,128)(2,1)} %x_hbm.1, s32[8,128]{1,0:T(8,128)} %bitcast.7, s32[8,128]{1,0:T(8,128)} %bitcast.8, f32[1,128]{1,0:T(1,128)} %constant.2.clone.freq_ref, bf16[2304]{0:T(1024)(128)(2,1)} %g_attn_pre.1, bf16[2304]{0:T(1024)(128)(2,1)} %g_attn_post.1, ...), custom_call_target="tpu_custom_call" | custom-call | tf_op jit(solution)/shard_map/step/pallas_call | solution.py:479
  171.8 4.5 %collect.1 = (f32[8,128]{1,0:T(8,128)}, bf16[1024,2304]{1,0:T(8,128)(2,1)}) custom-call(f32[2,16,8,128]{3,2,1,0:T(8,128)} %get-tuple-element.6.stats_hbm, bf16[1024,2304]{1,0:T(8,128)(2,1)} %get-tuple-element.7.y_hbm), custom_call_target="tpu_custom_call" | custom-call | tf_op jit(solution)/shard_map/collect/pallas_call | solution.py:458
